TPU v7x, 128 devices: a whole 4x4x4 slice. The times are simulated.
128 devices in a mesh: fsdp: 16 (over z, y), model: 8 (over x, core).
Axes of the slice: x: 4, y: 4, z: 4, core: 2. Of those that a mesh axis runs over, the one named last changes fastest.
Arguments:
- x_in: bfloat16 [128, 64, 4096], P('fsdp', 'model')
- gain_attn: float32 [2, 4096], replicated
- gain_mlp: float32 [2, 4096], replicated
- rope_cos: float32 [64, 64], replicated
- rope_sin: float32 [64, 64], replicated
- w_q: bfloat16 [2, 4096, 4096], P(None, 'fsdp', 'model')
- w_k: bfloat16 [2, 4096, 1024], P(None, 'fsdp', 'model')
- w_v: bfloat16 [2, 4096, 1024], P(None, 'fsdp', 'model')
- w_o: bfloat16 [2, 4096, 4096], P(None, 'model', 'fsdp')
- w_gate: bfloat16 [2, 4096, 14336], P(None, 'fsdp', 'model')
- w_up: bfloat16 [2, 4096, 14336], P(None, 'fsdp', 'model')
- w_down: bfloat16 [2, 14336, 4096], P(None, 'model', 'fsdp')
Outputs:
- output: bfloat16 [128, 64, 4096], P('fsdp', 'model')
All inputs are finite; a program needn't handle non-finite values.
Results may differ from a plain program's by a relative error of at most 0.02.
Values are sent between devices in bfloat16 or wider.
A program may use at most 1 GiB of HBM per device.

v0:
```python
import jax
import jax.numpy as jnp
from jax import lax
from jax.sharding import PartitionSpec as P

EPS = 1e-5


def rms_norm(seq_rows, gain_vec):
    rows_f = seq_rows.astype(jnp.float32)
    mean_sq = jnp.mean(rows_f * rows_f, axis=-1, keepdims=True)
    return (rows_f * lax.rsqrt(mean_sq + EPS) * gain_vec).astype(jnp.bfloat16)


def rotate(head_vals, cos_b, sin_b):
    half_dim = head_vals.shape[-1] // 2
    heads_f = head_vals.astype(jnp.float32)
    first_half = heads_f[..., :half_dim]
    second_half = heads_f[..., half_dim:]
    return jnp.concatenate([first_half * cos_b - second_half * sin_b, second_half * cos_b + first_half * sin_b], axis=-1).astype(jnp.bfloat16)


def attend(q_proj, k_proj, v_proj, rope_cos, rope_sin, kv_count):
    batch_rows, seq_len, q_width = q_proj.shape
    head_dim = 2 * rope_cos.shape[1]
    group_size = q_width // (head_dim * kv_count)
    q_rot = rotate(q_proj.reshape(batch_rows, seq_len, kv_count, group_size, head_dim), rope_cos[None, :, None, None, :], rope_sin[None, :, None, None, :])
    k_rot = rotate(k_proj.reshape(batch_rows, seq_len, kv_count, head_dim), rope_cos[None, :, None, :], rope_sin[None, :, None, :])
    v_heads = v_proj.reshape(batch_rows, seq_len, kv_count, head_dim)
    scores = jnp.einsum('bqkgd,bskd->bkgqs', q_rot, k_rot, preferred_element_type=jnp.float32) * head_dim ** -0.5
    positions = jnp.arange(seq_len)
    causal = positions[:, None] >= positions[None, :]
    scores = jnp.where(causal, scores, -jnp.inf)
    attn_probs = jax.nn.softmax(scores, axis=-1).astype(jnp.bfloat16)
    attn_out = jnp.einsum('bkgqs,bskd->bqkgd', attn_probs, v_heads, preferred_element_type=jnp.float32).astype(jnp.bfloat16)
    return attn_out.reshape(batch_rows, seq_len, q_width)


def solution(mesh):
    act_spec = P('fsdp', 'model', None)
    col_spec = P(None, 'fsdp', 'model')
    row_spec = P(None, 'model', 'fsdp')

    def device_step(x_in, gain_attn, gain_mlp, rope_cos, rope_sin, w_q, w_k, w_v, w_o, w_gate, w_up, w_down):
        head_dim = 2 * rope_cos.shape[1]
        kv_local = w_k.shape[-1] // head_dim
        residual = x_in
        for layer_idx in range(w_q.shape[0]):
            wq_full = lax.all_gather(w_q[layer_idx], 'fsdp', axis=0, tiled=True)
            wk_full = lax.all_gather(w_k[layer_idx], 'fsdp', axis=0, tiled=True)
            wv_full = lax.all_gather(w_v[layer_idx], 'fsdp', axis=0, tiled=True)
            wo_full = lax.all_gather(w_o[layer_idx], 'fsdp', axis=1, tiled=True)
            normed = rms_norm(residual, gain_attn[layer_idx])
            normed_all = lax.all_gather(normed, 'model', axis=1, tiled=True)
            q_proj = jnp.einsum('bsd,dn->bsn', normed_all, wq_full, preferred_element_type=jnp.float32).astype(jnp.bfloat16)
            k_proj = jnp.einsum('bsd,dn->bsn', normed_all, wk_full, preferred_element_type=jnp.float32).astype(jnp.bfloat16)
            v_proj = jnp.einsum('bsd,dn->bsn', normed_all, wv_full, preferred_element_type=jnp.float32).astype(jnp.bfloat16)
            attn_out = attend(q_proj, k_proj, v_proj, rope_cos, rope_sin, kv_local)
            attn_part = jnp.einsum('bsn,nd->bsd', attn_out, wo_full, preferred_element_type=jnp.float32)
            attn_sum = lax.psum_scatter(attn_part, 'model', scatter_dimension=1, tiled=True)
            mid_rows = (residual.astype(jnp.float32) + attn_sum).astype(jnp.bfloat16)
            wg_full = lax.all_gather(w_gate[layer_idx], 'fsdp', axis=0, tiled=True)
            wu_full = lax.all_gather(w_up[layer_idx], 'fsdp', axis=0, tiled=True)
            wd_full = lax.all_gather(w_down[layer_idx], 'fsdp', axis=1, tiled=True)
            normed_mlp = rms_norm(mid_rows, gain_mlp[layer_idx])
            mlp_in = lax.all_gather(normed_mlp, 'model', axis=1, tiled=True)
            gate_acc = jnp.einsum('bsd,df->bsf', mlp_in, wg_full, preferred_element_type=jnp.float32)
            up_acc = jnp.einsum('bsd,df->bsf', mlp_in, wu_full, preferred_element_type=jnp.float32)
            hidden = (jax.nn.silu(gate_acc) * up_acc).astype(jnp.bfloat16)
            mlp_part = jnp.einsum('bsf,fd->bsd', hidden, wd_full, preferred_element_type=jnp.float32)
            mlp_sum = lax.psum_scatter(mlp_part, 'model', scatter_dimension=1, tiled=True)
            residual = (mid_rows.astype(jnp.float32) + mlp_sum).astype(jnp.bfloat16)
        return residual

    return jax.shard_map(device_step, mesh=mesh, in_specs=(act_spec, P(), P(), P(), P(), col_spec, col_spec, col_spec, row_spec, col_spec, col_spec, row_spec), out_specs=act_spec, check_vma=False)
```

profile of v0, /device:TPU:1, one launch (start us, length us, event | category | flops | bytes accessed | tf_op | source)
XLA Modules:
  0.0 1463.6 jit_solution(12472716723028234827)
XLA Ops:
  16.9 36.5 %all-gather.43.cloned.1.call-done = bf16[1,4096,128]{2,1,0:T(8,128)(2,1)} async-done(((bf16[1,256,128]{2,1,0:T(8,128)(2,1)}), bf16[1,4096,128]{2,1,0:T(8,128)(2,1)}) %all-gather.43.cloned.1.call-update) | async-done | bytes 1048592 | tf_op jit(solution)/shard_map/all_gather | solution.py:50
  53.4 34.9 %all-gather.33.cloned.1.call-done = bf16[8,64,4096]{2,1,0:T(8,128)(2,1)} async-done(((bf16[8,8,4096]{2,1,0:T(8,128)(2,1)}), bf16[8,64,4096]{2,1,0:T(8,128)(2,1)}) %all-gather.33.cloned.1.call-update) | async-done | bytes 4194320 | tf_op jit(solution)/shard_map/all_gather | solution.py:54
  92.2 48.8 %all-gather.45.cloned.1.call-done = bf16[1,4096,512]{2,1,0:T(8,128)(2,1)} async-done(((bf16[1,256,512]{2,1,0:T(8,128)(2,1)}), bf16[1,4096,512]{2,1,0:T(8,128)(2,1)}) %all-gather.45.cloned.1.call-update) | async-done | bytes 4194320 | tf_op jit(solution)/shard_map/all_gather | solution.py:49
  149.1 34.4 %all-gather.41.cloned.1.call-done = bf16[1,4096,128]{2,1,0:T(8,128)(2,1)} async-done(((bf16[1,256,128]{2,1,0:T(8,128)(2,1)}), bf16[1,4096,128]{2,1,0:T(8,128)(2,1)}) %all-gather.41.cloned.1.call-update) | async-done | bytes 1048592 | tf_op jit(solution)/shard_map/all_gather | solution.py:51
  188.2 53.2 %all-gather.47.cloned.1.call-done = bf16[1,512,4096]{2,1,0:T(8,128)(2,1)} async-done(((bf16[1,512,256]{2,1,0:T(8,128)(2,1)}), bf16[1,512,4096]{2,1,0:T(8,128)(2,1)}) %all-gather.47.cloned.1.call-update) | async-done | bytes 4194320 | tf_op jit(solution)/shard_map/all_gather | solution.py:52
  252.2 49.8 %reduce-scatter.5.cloned.1.call-done = f32[8,8,4096]{2,1,0:T(8,128)} async-done(((f32[8,64,4096]{2,1,0:T(8,128)}), f32[8,8,4096]{2,1,0:T(8,128)}) %reduce-scatter.5.cloned.1.call-update) | async-done | bytes 1048592 | tf_op jit(solution)/shard_map/reduce_scatter | solution.py:60
  319.1 85.3 %all-gather.49.cloned.1.call-done = bf16[1,4096,1792]{2,1,0:T(8,128)(2,1)} async-done(((bf16[1,256,1792]{2,1,0:T(8,128)(2,1)}), bf16[1,4096,1792]{2,1,0:T(8,128)(2,1)}) %all-gather.49.cloned.1.call-update) | async-done | bytes 14680080 | tf_op jit(solution)/shard_map/all_gather | solution.py:62
  404.4 33.7 %all-gather.35.cloned.1.call-done = bf16[8,64,4096]{2,1,0:T(8,128)(2,1)} async-done(((bf16[8,8,4096]{2,1,0:T(8,128)(2,1)}), bf16[8,64,4096]{2,1,0:T(8,128)(2,1)}) %all-gather.35.cloned.1.call-update) | async-done | bytes 4194320 | tf_op jit(solution)/shard_map/all_gather | solution.py:66
  452.8 87.1 %all-gather.51.cloned.1.call-done = bf16[1,4096,1792]{2,1,0:T(8,128)(2,1)} async-done(((bf16[1,256,1792]{2,1,0:T(8,128)(2,1)}), bf16[1,4096,1792]{2,1,0:T(8,128)(2,1)}) %all-gather.51.cloned.1.call-update) | async-done | bytes 14680080 | tf_op jit(solution)/shard_map/all_gather | solution.py:63
  539.9 108.6 %all-gather.53.cloned.1.call-done = bf16[1,1792,4096]{2,1,0:T(8,128)(2,1)} async-done(((bf16[1,1792,256]{2,1,0:T(8,128)(2,1)}), bf16[1,1792,4096]{2,1,0:T(8,128)(2,1)}) %all-gather.53.cloned.1.call-update) | async-done | bytes 14680080 | tf_op jit(solution)/shard_map/all_gather | solution.py:64
  648.5 31.3 %fusion.6 = f32[8,64,4096]{2,1,0:T(8,128)} fusion(bf16[1,1792,4096]{2,1,0:T(8,128)(2,1)} %all-gather.53.cloned.1.call-done, f32[8,64,1792]{2,1,0:T(8,128)} %fusion.10, bf16[8,64,4096]{2,1,0:T(8,128)(2,1)} %all-gather.35.cloned.1.call-done, bf16[1,4096,1792]{2,1,0:T(8,128)(2,1)} %all-gather.51.cloned.1.call-done), kind=kOutput, calls=%fused_computation.6 | convolution fusion | flops 15037890560 | bytes 45613056 | tf_op jit(solution)/shard_map/bsf,fd->bsd/dot_general | solution.py:70
  680.8 51.8 %reduce-scatter.7.cloned.1.call-done = f32[8,8,4096]{2,1,0:T(8,128)} async-done(((f32[8,64,4096]{2,1,0:T(8,128)}), f32[8,8,4096]{2,1,0:T(8,128)}) %reduce-scatter.7.cloned.1.call-update) | async-done | bytes 1048592 | tf_op jit(solution)/shard_map/reduce_scatter | solution.py:71
  736.9 48.9 %all-gather.59.cloned.1.call-done = bf16[1,4096,512]{2,1,0:T(8,128)(2,1)} async-done(((bf16[1,256,512]{2,1,0:T(8,128)(2,1)}), bf16[1,4096,512]{2,1,0:T(8,128)(2,1)}) %all-gather.59.cloned.1.call-update) | async-done | bytes 4194320 | tf_op jit(solution)/shard_map/all_gather | solution.py:49
  785.8 33.7 %all-gather.37.cloned.1.call-done = bf16[8,64,4096]{2,1,0:T(8,128)(2,1)} async-done(((bf16[8,8,4096]{2,1,0:T(8,128)(2,1)}), bf16[8,64,4096]{2,1,0:T(8,128)(2,1)}) %all-gather.37.cloned.1.call-update) | async-done | bytes 4194320 | tf_op jit(solution)/shard_map/all_gather | solution.py:54
  825.6 36.1 %all-gather.57.cloned.1.call-done = bf16[1,4096,128]{2,1,0:T(8,128)(2,1)} async-done(((bf16[1,256,128]{2,1,0:T(8,128)(2,1)}), bf16[1,4096,128]{2,1,0:T(8,128)(2,1)}) %all-gather.57.cloned.1.call-update) | async-done | bytes 1048592 | tf_op jit(solution)/shard_map/all_gather | solution.py:50
  867.6 37.8 %all-gather.55.cloned.1.call-done = bf16[1,4096,128]{2,1,0:T(8,128)(2,1)} async-done(((bf16[1,256,128]{2,1,0:T(8,128)(2,1)}), bf16[1,4096,128]{2,1,0:T(8,128)(2,1)}) %all-gather.55.cloned.1.call-update) | async-done | bytes 1048592 | tf_op jit(solution)/shard_map/all_gather | solution.py:51
  910.2 53.2 %all-gather.61.cloned.1.call-done = bf16[1,512,4096]{2,1,0:T(8,128)(2,1)} async-done(((bf16[1,512,256]{2,1,0:T(8,128)(2,1)}), bf16[1,512,4096]{2,1,0:T(8,128)(2,1)}) %all-gather.61.cloned.1.call-update) | async-done | bytes 4194320 | tf_op jit(solution)/shard_map/all_gather | solution.py:52
  971.8 52.2 %reduce-scatter.9.cloned.1.call-done = f32[8,8,4096]{2,1,0:T(8,128)} async-done(((f32[8,64,4096]{2,1,0:T(8,128)}), f32[8,8,4096]{2,1,0:T(8,128)}) %reduce-scatter.9.cloned.1.call-update) | async-done | bytes 1048592 | tf_op jit(solution)/shard_map/reduce_scatter | solution.py:60
  1027.8 98.4 %all-gather.63.cloned.1.call-done = bf16[1,4096,1792]{2,1,0:T(8,128)(2,1)} async-done(((bf16[1,256,1792]{2,1,0:T(8,128)(2,1)}), bf16[1,4096,1792]{2,1,0:T(8,128)(2,1)}) %all-gather.63.cloned.1.call-update) | async-done | bytes 14680080 | tf_op jit(solution)/shard_map/all_gather | solution.py:62
  1126.2 33.7 %all-gather.39.cloned.1.call-done = bf16[8,64,4096]{2,1,0:T(8,128)(2,1)} async-done(((bf16[8,8,4096]{2,1,0:T(8,128)(2,1)}), bf16[8,64,4096]{2,1,0:T(8,128)(2,1)}) %all-gather.39.cloned.1.call-update) | async-done | bytes 4194320 | tf_op jit(solution)/shard_map/all_gather | solution.py:66
  1174.7 86.9 %all-gather.65.cloned.1.call-done = bf16[1,4096,1792]{2,1,0:T(8,128)(2,1)} async-done(((bf16[1,256,1792]{2,1,0:T(8,128)(2,1)}), bf16[1,4096,1792]{2,1,0:T(8,128)(2,1)}) %all-gather.65.cloned.1.call-update) | async-done | bytes 14680080 | tf_op jit(solution)/shard_map/all_gather | solution.py:63
  1261.6 108.8 %all-gather.67.cloned.1.call-done = bf16[1,1792,4096]{2,1,0:T(8,128)(2,1)} async-done(((bf16[1,1792,256]{2,1,0:T(8,128)(2,1)}), bf16[1,1792,4096]{2,1,0:T(8,128)(2,1)}) %all-gather.67.cloned.1.call-update) | async-done | bytes 14680080 | tf_op jit(solution)/shard_map/all_gather | solution.py:64
  1370.3 31.3 %fusion = f32[8,64,4096]{2,1,0:T(8,128)} fusion(bf16[1,1792,4096]{2,1,0:T(8,128)(2,1)} %all-gather.67.cloned.1.call-done, f32[8,64,1792]{2,1,0:T(8,128)} %fusion.4, bf16[8,64,4096]{2,1,0:T(8,128)(2,1)} %all-gather.39.cloned.1.call-done, bf16[1,4096,1792]{2,1,0:T(8,128)(2,1)} %all-gather.65.cloned.1.call-done), kind=kOutput, calls=%fused_computation | convolution fusion | flops 15037890560 | bytes 45613056 | tf_op jit(solution)/shard_map/bsf,fd->bsd/dot_general | solution.py:70
  1401.7 52.8 %reduce-scatter.11.cloned.1.call-done = f32[8,8,4096]{2,1,0:T(8,128)} async-done(((f32[8,64,4096]{2,1,0:T(8,128)}), f32[8,8,4096]{2,1,0:T(8,128)}) %reduce-scatter.11.cloned.1.call-update) | async-done | bytes 1048592 | tf_op jit(solution)/shard_map/reduce_scatter | solution.py:71
  (107 shorter events, 120.4 us)
Async XLA Ops:
  6.5 46.8 %all-gather.43.cloned.1.call-start = ((), (), s32[]{:S(2)}) async-start(), calls=%async_computation.13 | async-start | bytes 1114112 | tf_op jit(solution)/shard_map/all_gather | solution.py:50
  8.2 80.1 %all-gather.33.cloned.1.call-start = ((), (), s32[]{:S(2)}) async-start(), calls=%async_computation.4 | async-start | bytes 4718592 | tf_op jit(solution)/shard_map/all_gather | solution.py:54
  12.4 128.6 %all-gather.45.cloned.1.call-start = ((), (), s32[]{:S(2)}) async-start(), calls=%async_computation.14 | async-start | bytes 4456448 | tf_op jit(solution)/shard_map/all_gather | solution.py:49
  14.3 169.1 %all-gather.41.cloned.1.call-start = ((), (), s32[]{:S(2)}) async-start(), calls=%async_computation.12 | async-start | bytes 1114112 | tf_op jit(solution)/shard_map/all_gather | solution.py:51
  15.9 225.5 %all-gather.47.cloned.1.call-start = ((), (), s32[]{:S(2)}) async-start(), calls=%async_computation.15 | async-start | bytes 4456448 | tf_op jit(solution)/shard_map/all_gather | solution.py:52
  16.8 285.2 %reduce-scatter.5.cloned.1.call-start = ((), (), s32[]{:S(2)}) async-start(), calls=%async_computation.5 | async-start | bytes 9437184 | tf_op jit(solution)/shard_map/reduce_scatter | solution.py:60
  16.9 75.1 %copy-start.3 = (f32[64,64]{1,0:T(8,128)S(1)}, f32[64,64]{1,0:T(8,128)}, u32[]{:S(2)}) copy-start(f32[64,64]{1,0:T(8,128)} %param.16) | copy-start | bytes 49156
  16.9 75.1 %copy-start.4 = (f32[64,64]{1,0:T(8,128)S(1)}, f32[64,64]{1,0:T(8,128)}, u32[]{:S(2)}) copy-start(f32[64,64]{1,0:T(8,128)} %param.15) | copy-start | bytes 49156
  249.3 155.2 %all-gather.49.cloned.1.call-start = ((), (), s32[]{:S(2)}) async-start(), calls=%async_computation.16 | async-start | bytes 15597568 | tf_op jit(solution)/shard_map/all_gather | solution.py:62
  252.1 186.0 %all-gather.35.cloned.1.call-start = ((), (), s32[]{:S(2)}) async-start(), calls=%async_computation.6 | async-start | bytes 4718592 | tf_op jit(solution)/shard_map/all_gather | solution.py:66
  304.5 235.4 %all-gather.51.cloned.1.call-start = ((), (), s32[]{:S(2)}) async-start(), calls=%async_computation.17 | async-start | bytes 15597568 | tf_op jit(solution)/shard_map/all_gather | solution.py:63
  306.0 342.6 %all-gather.53.cloned.1.call-start = ((), (), s32[]{:S(2)}) async-start(), calls=%async_computation.18 | async-start | bytes 15597568 | tf_op jit(solution)/shard_map/all_gather | solution.py:64
  308.9 423.7 %reduce-scatter.7.cloned.1.call-start = ((), (), s32[]{:S(2)}) async-start(), calls=%async_computation.7 | async-start | bytes 9437184 | tf_op jit(solution)/shard_map/reduce_scatter | solution.py:71
  679.8 105.9 %all-gather.59.cloned.1.call-start = ((), (), s32[]{:S(2)}) async-start(), calls=%async_computation.21 | async-start | bytes 4456448 | tf_op jit(solution)/shard_map/all_gather | solution.py:49
  680.4 139.1 %all-gather.37.cloned.1.call-start = ((), (), s32[]{:S(2)}) async-start(), calls=%async_computation.8 | async-start | bytes 4718592 | tf_op jit(solution)/shard_map/all_gather | solution.py:54
  735.1 126.6 %all-gather.57.cloned.1.call-start = ((), (), s32[]{:S(2)}) async-start(), calls=%async_computation.20 | async-start | bytes 1114112 | tf_op jit(solution)/shard_map/all_gather | solution.py:50
  735.7 169.7 %all-gather.55.cloned.1.call-start = ((), (), s32[]{:S(2)}) async-start(), calls=%async_computation.19 | async-start | bytes 1114112 | tf_op jit(solution)/shard_map/all_gather | solution.py:51
  736.3 227.1 %all-gather.61.cloned.1.call-start = ((), (), s32[]{:S(2)}) async-start(), calls=%async_computation.22 | async-start | bytes 4456448 | tf_op jit(solution)/shard_map/all_gather | solution.py:52
  736.8 287.1 %reduce-scatter.9.cloned.1.call-start = ((), (), s32[]{:S(2)}) async-start(), calls=%async_computation.9 | async-start | bytes 9437184 | tf_op jit(solution)/shard_map/reduce_scatter | solution.py:60
  971.2 155.0 %all-gather.63.cloned.1.call-start = ((), (), s32[]{:S(2)}) async-start(), calls=%async_computation.23 | async-start | bytes 15597568 | tf_op jit(solution)/shard_map/all_gather | solution.py:62
  971.8 188.2 %all-gather.39.cloned.1.call-start = ((), (), s32[]{:S(2)}) async-start(), calls=%async_computation.10 | async-start | bytes 4718592 | tf_op jit(solution)/shard_map/all_gather | solution.py:66
  1026.5 235.1 %all-gather.65.cloned.1.call-start = ((), (), s32[]{:S(2)}) async-start(), calls=%async_computation.24 | async-start | bytes 15597568 | tf_op jit(solution)/shard_map/all_gather | solution.py:63
  1027.1 343.3 %all-gather.67.cloned.1.call-start = ((), (), s32[]{:S(2)}) async-start(), calls=%async_computation.25 | async-start | bytes 15597568 | tf_op jit(solution)/shard_map/all_gather | solution.py:64
  1027.8 426.7 %reduce-scatter.11.cloned.1.call-start = ((), (), s32[]{:S(2)}) async-start(), calls=%async_computation.11 | async-start | bytes 9437184 | tf_op jit(solution)/shard_map/reduce_scatter | solution.py:71
  (5 other events, 119.1 us)
Sparse Core Ops, SparseCore 0:
  9.5 43.8 all-gather.42
  55.0 33.1 all-gather.32
  90.4 50.4 all-gather.44
  142.9 40.4 all-gather.40
  185.4 55.9 all-gather.46
  249.4 52.6 reduce-scatter.4
  304.2 100.1 all-gather.48
  406.1 31.9 all-gather.34
  440.3 99.5 all-gather.50
  541.9 106.6 all-gather.52
  679.9 52.6 reduce-scatter.6
  734.6 51.1 all-gather.58
  787.5 31.9 all-gather.36
  821.5 40.1 all-gather.56
  863.7 41.6 all-gather.54
  907.4 55.9 all-gather.60
  971.3 52.6 reduce-scatter.8
  1026.0 100.1 all-gather.62
  1127.9 31.9 all-gather.38
  1161.9 99.5 all-gather.64
  1263.7 106.6 all-gather.66
  1401.8 52.6 reduce-scatter.10
where the time goes:
time: 1470 us; the launch traced here: 1460 us
  waiting for transfers between devices  1270 us (86%)
  matrix products  136 us (9%)
  local copies, waits for them, and re-layouts  16.9 us (1%)
    all_gather x2, waiting for transfers between devices, device_step(): wd_full = lax.all_gather(w_down[layer_idx], 'fsdp', axis=1, tiled=True)  217 us
    all_gather x2, waiting for transfers between devices, device_step(): wg_full = lax.all_gather(w_gate[layer_idx], 'fsdp', axis=0, tiled=True)  184 us
    all_gather x2, waiting for transfers between devices, device_step(): wu_full = lax.all_gather(w_up[layer_idx], 'fsdp', axis=0, tiled=True)  174 us
    all_gather x2, waiting for transfers between devices, device_step(): wo_full = lax.all_gather(w_o[layer_idx], 'fsdp', axis=1, tiled=True)  106 us
    reduce_scatter x2, waiting for transfers between devices, device_step(): lax.psum_scatter(mlp_part, 'model', scatter_dimension=1, tiled=True)  105 us
    reduce_scatter x2, waiting for transfers between devices, device_step(): lax.psum_scatter(attn_part, 'model', scatter_dimension=1, tiled=True)  102 us
    all_gather x2, waiting for transfers between devices, device_step(): wq_full = lax.all_gather(w_q[layer_idx], 'fsdp', axis=0, tiled=True)  97.7 us
    all_gather x2, waiting for transfers between devices, device_step(): wk_full = lax.all_gather(w_k[layer_idx], 'fsdp', axis=0, tiled=True)  72.5 us
  transfers between devices with their start and end apart: 22, of which 22 were waited for; matrix products, arithmetic and copies ran while one was open for 6% of the time, Pallas kernels for 0%

commit v1 on v0

v1 whole, which is shorter than its diff:
```python
import functools
import jax
import jax.numpy as jnp
from jax import lax
from jax.experimental import pallas as pl
from jax.experimental.pallas import tpu as pltpu
from jax.sharding import PartitionSpec as P

EPS = 1e-5
MESH = pl.DeviceIdType.MESH
FULL = slice(None)

UNITS = 26
ITEMS = 13
N_ITEMS = 2 * ITEMS
KV = 2
O_BASE = 3
GU_BASE = 5
D_BASE = 19
RING = 4
LANE = 128
UNIT = 256
ROWS = 512
TOK = 64
HEAD_SCALE = 128 ** -0.5
BOTH = (0, 1)
SIGNS = (1, -1)


def _plan():
    plan = []

    def add(stage, src, sub, half, axis, sign):
        dst = list(src)
        dst[axis] -= sign
        rel = [(v[0] % RING) * RING + v[1] % RING for v in (src, dst)]
        quarters = {(a, b) for a in BOTH for b in BOTH if sub in (a, None) and half in (b, None)}
        plan.append(dict(stage=stage, src=rel[0], dst=rel[1], sub=sub, half=half, dir=(axis, sign), q=quarters))

    for axis in BOTH:
        for sign in SIGNS:
            sub = (1 - sign) // 2

            def at(along, across):
                return (along, across) if axis == 0 else (across, along)

            add(0, at(0, 0), None, None, axis, sign)
            add(1, at(-sign, 0), sub, None, axis, sign)
            for k in SIGNS:
                add(1, at(0, k), None, axis, axis, sign)
                add(2, at(-sign, k), sub, axis, axis, sign)
            add(2, at(0, 2), None, axis, axis, sign)
            add(3, at(-sign, 2), sub, axis, axis, sign)
    return plan


PLAN = _plan()
N_COPY = len(PLAN)


def _pick(sub, half):
    return (FULL if sub is None else pl.ds(sub, 1), FULL if half is None else pl.ds(half, 1))


def body(x_ref, ga_ref, gm_ref, cos_ref, sin_ref, wq, wk, wv, wo, wg, wu, wd, y_ref, g_ref,
         hu, wbuf, dbuf, part, t1, t2, t3, zbuf, qbuf, kbuf, vbuf, obuf, res, acc_a, acc_b,
         st_recv, st_send, ag_recv, ag_send, rs_recv, rs_send, w_sem, d_sem):
    f_me = lax.axis_index("fsdp")
    m_me = lax.axis_index("model")
    z, y = lax.div(f_me, 4), lax.rem(f_me, 4)
    x, c = lax.div(m_me, 2), lax.rem(m_me, 2)
    up = lambda v: lax.rem(v + 1, 4)
    dn = lambda v: lax.rem(v + 3, 4)
    sib = 1 - c

    dev_of = {}
    for s, turn in zip(SIGNS, (up, dn)):
        dev_of[0, s] = (turn(z) * 4 + y, m_me)
        dev_of[1, s] = (z * 4 + turn(y), m_me)
    x_up, x_dn, x_far = up(x), dn(x), lax.rem(x + 2, 4)
    dev_xu, dev_xd, dev_sib = (f_me, x_up * 2 + c), (f_me, x_dn * 2 + c), (f_me, x * 2 + sib)

    def stream_copy(item, i):
        p = PLAN[i]
        a, b = _pick(p["sub"], p["half"])
        u = pl.ds(2 * item, 2)
        at = p["src"] if p["stage"] else p["dst"]
        src = g_ref.at[u, at, a, b]
        return pltpu.make_async_remote_copy(
            src_ref=src, dst_ref=g_ref.at[u, p["dst"], a, b],
            send_sem=st_send.at[item], recv_sem=st_recv.at[item, i],
            device_id=dev_of[p["dir"]], device_id_type=MESH)

    def arrivals(stage):
        return [i for i in range(N_COPY) if PLAN[i]["stage"] == stage]

    def start_unit(item, e):
        unit = 2 * item + e
        layer, ul = lax.div(unit, UNITS), lax.rem(unit, UNITS)

        def send(src, lane=None):
            for i in arrivals(0):
                dst = g_ref.at[unit, PLAN[i]["dst"]]
                pltpu.make_async_remote_copy(
                    src_ref=src, dst_ref=dst if lane is None else dst.at[:, :, :, pl.ds(lane, LANE)],
                    send_sem=st_send.at[item], recv_sem=st_recv.at[item, i],
                    device_id=dev_of[PLAN[i]["dir"]], device_id_type=MESH).start()

        @pl.when(ul < KV)
        def _():
            send(own_cols(wq, layer, ul))

        @pl.when(ul == KV)
        def _():
            send(wk.at[layer], 0)
            send(wv.at[layer], LANE)

        for w, lo, hi, n_row in ((wo, O_BASE, GU_BASE, 2), (wd, D_BASE, UNITS, 7)):
            @pl.when(jnp.logical_and(ul >= lo, ul < hi))
            def _():
                for k in BOTH:
                    send(own_part(w, layer, n_row, 2 * (ul - lo) + k), k * LANE)

        for k, w in enumerate((wg, wu)):
            @pl.when(jnp.logical_and(jnp.logical_and(ul >= GU_BASE, ul < D_BASE), lax.rem(ul - GU_BASE, 2) == k))
            def _():
                send(own_cols(w, layer, lax.div(ul - GU_BASE, 2)))

    def own_cols(w, layer, j):
        return w.at[layer, :, :, :, pl.ds(pl.multiple_of(j * UNIT, UNIT), UNIT)]

    def own_part(w, layer, n_row, s):
        lane = pl.multiple_of(lax.div(s, n_row) * LANE, LANE)
        return w.at[layer, lax.rem(s, n_row), :, :, :, pl.ds(lane, LANE)]

    def start_own(item):
        for e in BOTH:
            start_unit(item, e)

    def forward(item, stage):
        waited = set()
        for i in arrivals(stage):
            p = PLAN[i]
            for j in arrivals(stage - 1):
                if j not in waited and PLAN[j]["dst"] == p["src"] and PLAN[j]["q"] & p["q"]:
                    stream_copy(item, j).wait_recv()
                    waited.add(j)
            stream_copy(item, i).start()
        for j in arrivals(stage - 1):
            if j not in waited:
                stream_copy(item, j).wait_recv()

    def tick(t):
        @pl.when(t < N_ITEMS)
        def _():
            forward(t, 1)

        @pl.when(jnp.logical_and(t >= 1, t < N_ITEMS + 1))
        def _():
            forward(t - 1, 2)

        @pl.when(jnp.logical_and(t >= 2, t < N_ITEMS + 2))
        def _():
            forward(t - 2, 3)

        @pl.when(t + 2 < N_ITEMS)
        def _():
            start_own(t + 2)

        @pl.when(jnp.logical_and(t >= 3, t < N_ITEMS + 3))
        def _():
            for j in arrivals(3):
                stream_copy(t - 3, j).wait_recv()

    def ag_copy(inst, k):
        slot = lax.rem(inst, 2)
        own, lo, hi, far = (x * 2 + c), (x_dn * 2 + c), (x_up * 2 + c), (x_far * 2 + c)
        s0, s1 = pl.ds(0, 32), pl.ds(32, 32)
        blk, rows, dev = [
            (own, FULL, dev_sib), (own, FULL, dev_xu), (own, FULL, dev_xd),
            (lo, s0, dev_xu), (hi, s1, dev_xd),
            (lo, FULL, dev_sib), (hi, FULL, dev_sib), (far, FULL, dev_sib)][k]
        return pltpu.make_async_remote_copy(
            src_ref=hu.at[slot, blk, rows], dst_ref=hu.at[slot, blk, rows],
            send_sem=ag_send.at[inst, k], recv_sem=ag_recv.at[inst, k], device_id=dev, device_id_type=MESH)

    def ag_start(inst):
        for k in (1, 2, 0):
            ag_copy(inst, k).start()

    def ag_mid(inst):
        ag_copy(inst, 1).wait_recv()
        ag_copy(inst, 3).start()
        ag_copy(inst, 5).start()
        ag_copy(inst, 2).wait_recv()
        ag_copy(inst, 4).start()
        ag_copy(inst, 6).start()

    def ag_end(inst):
        ag_copy(inst, 3).wait_recv()
        ag_copy(inst, 4).wait_recv()
        ag_copy(inst, 7).start()
        for k in (0, 5, 6, 7):
            ag_copy(inst, k).wait_recv()
        for k in range(8):
            ag_copy(inst, k).wait_send()

    def rs_copy(inst, hh, k):
        lo, hi = pl.ds(0, 32), pl.ds(32, 32)
        src, dst, dev = [
            (part.at[hh, :, sib], t1.at[hh], dev_sib),
            (part.at[hh, x_far, c, lo], t2.at[hh, 0], dev_xu),
            (part.at[hh, x_far, c, hi], t2.at[hh, 1], dev_xd),
            (part.at[hh, x_up, c], t3.at[hh, 0], dev_xu),
            (part.at[hh, x_dn, c], t3.at[hh, 1], dev_xd)][k]
        return pltpu.make_async_remote_copy(
            src_ref=src, dst_ref=dst, send_sem=rs_send.at[inst, hh, k], recv_sem=rs_recv.at[inst, hh, k],
            device_id=dev, device_id_type=MESH)

    def rs_core(inst, hh):
        rs_copy(inst, hh, 0).start()

    def rs_far(inst, hh):
        rs_copy(inst, hh, 0).wait_recv()

        def add(xp):
            part[hh, xp, c] = part[hh, xp, c] + t1[hh, xp]

        add(x_far)
        rs_copy(inst, hh, 1).start()
        rs_copy(inst, hh, 2).start()
        for xp in (x_up, x_dn, x):
            add(xp)

    def rs_near(inst, hh):
        rs_copy(inst, hh, 1).wait_recv()
        part[hh, x_up, c, 0:32] = part[hh, x_up, c, 0:32] + t2[hh, 0]
        rs_copy(inst, hh, 3).start()
        rs_copy(inst, hh, 2).wait_recv()
        part[hh, x_dn, c, 32:TOK] = part[hh, x_dn, c, 32:TOK] + t2[hh, 1]
        rs_copy(inst, hh, 4).start()

    def rs_wait(inst, hh):
        rs_copy(inst, hh, 3).wait_recv()
        rs_copy(inst, hh, 4).wait_recv()
        for k in range(5):
            rs_copy(inst, hh, k).wait_send()

    def add_residual():
        def rows16(i, _):
            r = pl.ds(pl.multiple_of(i * 16, 16), 16)
            s = [part[hh, x, c, r] + t3[hh, 0, r] + t3[hh, 1, r] for hh in range(2)]
            cols = []
            for f in range(16):
                for hh in range(2):
                    cols.append(s[hh][:, f * LANE:(f + 1) * LANE])
            total = jnp.concatenate(cols, axis=1)
            res[r] = (res[r].astype(jnp.float32) + total).astype(jnp.bfloat16)
            return 0
        lax.fori_loop(0, 4, rows16, 0)

    def norm_into(slot, gain):
        def rows16(i, _):
            r = pl.ds(pl.multiple_of(i * 16, 16), 16)
            v = res[r].astype(jnp.float32)
            ms = jnp.mean(v * v, axis=-1, keepdims=True)
            hu[slot, m_me, r] = (v * lax.rsqrt(ms + EPS) * gain).astype(jnp.bfloat16)
            return 0
        lax.fori_loop(0, 4, rows16, 0)

    def abs_of(rel):
        return lax.rem(z + lax.div(rel, 4), 4) * 4 + lax.rem(y + lax.rem(rel, 4), 4)

    def load_unit(unit, slot, own):
        mine = wbuf.at[slot, f_me]
        if len(own) == 1:
            pltpu.make_async_copy(own[0], mine, w_sem.at[slot]).start()
        else:
            for k in BOTH:
                pltpu.make_async_copy(own[k], mine.at[:, :, :, pl.ds(k * LANE, LANE)], w_sem.at[slot]).start()

        def one(rel, _):
            pltpu.make_async_copy(g_ref.at[unit, rel], wbuf.at[slot, abs_of(rel)], w_sem.at[slot]).start()
            return 0
        lax.fori_loop(1, 16, one, 0)

    def wait_unit(slot):
        pltpu.make_async_copy(wbuf.at[slot], wbuf.at[slot], w_sem.at[slot]).wait()

    def load_cols(w, layer, base, n_row, hh):
        def row(r, _):
            s = hh * n_row + r
            unit = layer * UNITS + base + lax.div(s, 2)
            lane = pl.ds(pl.multiple_of(lax.rem(s, 2) * LANE, LANE), LANE)

            def dst(f):
                return dbuf.at[r, :, :, :, pl.ds(pl.multiple_of(f * LANE, LANE), LANE)]
            pltpu.make_async_copy(own_part(w, layer, n_row, s), dst(f_me), d_sem).start()

            def one(rel, _):
                pltpu.make_async_copy(g_ref.at[unit, rel, :, :, :, lane], dst(abs_of(rel)), d_sem).start()
                return 0
            lax.fori_loop(1, 16, one, 0)
            return 0
        lax.fori_loop(0, n_row, row, 0)
        span = dbuf.at[pl.ds(0, n_row)]
        pltpu.make_async_copy(span, span, d_sem).wait()

    def project(slot, wslots, accs):
        for acc in accs:
            acc[...] = jnp.zeros_like(acc)

        def step(kk, _):
            lhs = hu[slot, :, :, pl.ds(pl.multiple_of(kk * ROWS, ROWS), ROWS)].reshape(ROWS, ROWS)
            for ws, acc in zip(wslots, accs):
                rhs = wbuf[ws, pl.ds(2 * kk, 2)].reshape(ROWS, UNIT)
                acc[...] += jnp.dot(lhs, rhs, preferred_element_type=jnp.float32)
            return 0
        lax.fori_loop(0, 8, step, 0)

    def rope_store(src, lane, dst):
        def rows(i, _):
            r = pl.ds(pl.multiple_of(i * LANE, LANE), LANE)
            v = src[r, lane:lane + LANE].astype(jnp.bfloat16).astype(jnp.float32)
            out = v * cos_ref[r] + pltpu.roll(v, TOK, 1) * sin_ref[r]
            dst[r] = out.astype(jnp.bfloat16)
            return 0
        lax.fori_loop(0, 4, rows, 0)

    def attention(layer):
        base = layer * UNITS
        slot = 0
        for u in BOTH:
            load_unit(base + u, u, [own_cols(wq, layer, u)])
        load_unit(base + KV, KV, [wk.at[layer], wv.at[layer]])
        wait_unit(0)
        wait_unit(1)
        project(slot, (0, 1), (acc_a, acc_b))
        for h in range(4):
            rope_store(acc_a if h < 2 else acc_b, (h % 2) * LANE, qbuf.at[h])
        wait_unit(2)
        project(slot, (2,), (acc_a,))
        rope_store(acc_a, 0, kbuf)
        vbuf[...] = acc_a[:, LANE:UNIT].astype(jnp.bfloat16)

        def rows(i, _):
            r0 = pl.multiple_of(i * LANE, LANE)
            r = pl.ds(r0, LANE)
            qi = lax.broadcasted_iota(jnp.int32, (LANE, ROWS), 0) + r0
            ki = lax.broadcasted_iota(jnp.int32, (LANE, ROWS), 1)
            same = ((qi >> 3) & 7) == ((ki >> 3) & 7)
            qpos = (qi >> 6) * 8 + (qi & 7)
            kpos = (ki >> 6) * 8 + (ki & 7)
            ok = jnp.logical_and(same, qpos >= kpos)
            for h in range(4):
                s = lax.dot_general(qbuf[h, r], kbuf[...], (((1,), (1,)), ((), ())), preferred_element_type=jnp.float32)
                s = jnp.where(ok, s * (HEAD_SCALE), -jnp.inf)
                e = jnp.exp(s - jnp.max(s, axis=-1, keepdims=True))
                p = (e / jnp.sum(e, axis=-1, keepdims=True)).astype(jnp.bfloat16)
                o = jnp.dot(p, vbuf[...], preferred_element_type=jnp.float32)
                obuf[r, h * LANE:(h + 1) * LANE] = o.astype(jnp.bfloat16)
            return 0
        lax.fori_loop(0, 4, rows, 0)

    def down(act, w, layer, n_row, base, hh):
        load_cols(w, layer, base, n_row, hh)

        def tile(n, _):
            cols = pl.ds(pl.multiple_of(n * UNIT, UNIT), UNIT)
            rhs = dbuf[0:n_row, :, :, :, cols].reshape(n_row * UNIT, UNIT)
            out = jnp.dot(act[...], rhs, preferred_element_type=jnp.float32)
            part[hh, :, :, :, cols] = out.reshape(4, 2, TOK, UNIT)
            return 0
        lax.fori_loop(0, 8, tile, 0)

    def gate_up(layer, j0, j1):
        def load(j, b):
            u = layer * UNITS + GU_BASE + 2 * j
            load_unit(u, 2 * b, [own_cols(wg, layer, j)])
            load_unit(u + 1, 2 * b + 1, [own_cols(wu, layer, j)])

        load(j0, j0 % 2)

        def step(j, _):
            b = lax.rem(j, 2)

            @pl.when(j + 1 < j1)
            def _():
                load(j + 1, 1 - b)
            wait_unit(2 * b)
            wait_unit(2 * b + 1)
            project(1, (2 * b, 2 * b + 1), (acc_a, acc_b))

            def rows(i, _):
                r = pl.ds(pl.multiple_of(i * LANE, LANE), LANE)
                hid = jax.nn.silu(acc_a[r]) * acc_b[r]
                zbuf[r, pl.ds(pl.multiple_of(j * UNIT, UNIT), UNIT)] = hid.astype(jnp.bfloat16)
                return 0
            lax.fori_loop(0, 4, rows, 0)
            return 0
        lax.fori_loop(j0, j1, step, 0)

    barrier = pltpu.get_barrier_semaphore()
    peers = list(dev_of.values()) + [dev_xu, dev_xd, dev_sib]
    for dev in peers:
        pl.semaphore_signal(barrier, inc=1, device_id=dev, device_id_type=MESH)
    pl.semaphore_wait(barrier, len(peers))

    start_own(0)
    start_own(1)
    res[...] = x_ref[...]
    norm_into(0, ga_ref[0])
    ag_start(0)

    def hooks(layer, tau):
        a_inst, m_inst = 2 * layer, 2 * layer + 1

        @pl.when(tau == 5)
        def _():
            ag_mid(a_inst)

        @pl.when(tau == 6)
        def _():
            ag_end(a_inst)
            attention(layer)
            for hh in range(2):
                down(obuf, wo, layer, 2, O_BASE, hh)
                rs_core(a_inst, hh)

        @pl.when(tau == 7)
        def _():
            for hh in range(2):
                rs_far(a_inst, hh)

        @pl.when(tau == 8)
        def _():
            for hh in range(2):
                rs_near(a_inst, hh)

        @pl.when(tau == 9)
        def _():
            for hh in range(2):
                rs_wait(a_inst, hh)
            add_residual()
            norm_into(1, gm_ref[layer])
            ag_start(m_inst)

        @pl.when(tau == 10)
        def _():
            ag_mid(m_inst)

        @pl.when(tau == 11)
        def _():
            ag_end(m_inst)
            gate_up(layer, 0, 6)

        @pl.when(tau == 12)
        def _():
            gate_up(layer, 6, 7)

        @pl.when(tau == 14)
        def _():
            down(zbuf, wd, layer, 7, D_BASE, 0)
            rs_core(m_inst, 0)

        @pl.when(tau == 15)
        def _():
            rs_far(m_inst, 0)
            down(zbuf, wd, layer, 7, D_BASE, 1)
            rs_core(m_inst, 1)

        @pl.when(tau == 16)
        def _():
            rs_near(m_inst, 0)
            rs_far(m_inst, 1)

        @pl.when(tau == 17)
        def _():
            rs_near(m_inst, 1)
            for hh in range(2):
                rs_wait(m_inst, hh)
            add_residual()

            @pl.when(layer == 0)
            def _():
                norm_into(0, ga_ref[1])
                ag_start(2)

    def step(t, _):
        tick(t)

        @pl.when(t >= 5)
        def _():
            hooks(lax.div(t - 5, ITEMS), lax.rem(t - 5, ITEMS) + 5)
        return 0
    lax.fori_loop(0, 5 + 2 * ITEMS, step, 0)
    y_ref[...] = res[...]

    def drain(i, _):
        span = g_ref.at[pl.ds(2 * i, 2), pl.ds(0, 15)]
        pltpu.make_async_copy(span, span, st_send.at[i]).wait()
        return 0
    lax.fori_loop(0, N_ITEMS, drain, 0)


def _call(x, ga, gm, cos, sin, *weights):
    bf, f32 = jnp.bfloat16, jnp.float32
    vm = pl.BlockSpec(memory_space=pltpu.VMEM)
    anys = pl.BlockSpec(memory_space=pl.ANY)
    return pl.pallas_call(
        body,
        out_shape=(jax.ShapeDtypeStruct((TOK, 4096), bf), jax.ShapeDtypeStruct((2 * UNITS, 16, 2, 2, TOK, UNIT), bf)),
        in_specs=[vm] * 5 + [anys] * len(weights),
        out_specs=(vm, anys),
        scratch_shapes=[
            pltpu.VMEM((2, 8, TOK, 4096), bf),
            pltpu.VMEM((4, 16, 2, 2, TOK, UNIT), bf),
            pltpu.VMEM((7, 2, 2, TOK, 2048), bf),
            pltpu.VMEM((2, 4, 2, TOK, 2048), f32),
            pltpu.VMEM((2, 4, TOK, 2048), f32),
            pltpu.VMEM((2, 2, 32, 2048), f32),
            pltpu.VMEM((2, 2, TOK, 2048), f32),
            pltpu.VMEM((ROWS, 1792), bf),
            pltpu.VMEM((4, ROWS, LANE), bf),
            pltpu.VMEM((ROWS, LANE), bf),
            pltpu.VMEM((ROWS, LANE), bf),
            pltpu.VMEM((ROWS, ROWS), bf),
            pltpu.VMEM((TOK, 4096), bf),
            pltpu.VMEM((ROWS, UNIT), f32),
            pltpu.VMEM((ROWS, UNIT), f32),
            pltpu.SemaphoreType.DMA((N_ITEMS, N_COPY)),
            pltpu.SemaphoreType.DMA((N_ITEMS,)),
            pltpu.SemaphoreType.DMA((4, 8)),
            pltpu.SemaphoreType.DMA((4, 8)),
            pltpu.SemaphoreType.DMA((4, 2, 5)),
            pltpu.SemaphoreType.DMA((4, 2, 5)),
            pltpu.SemaphoreType.DMA((4,)),
            pltpu.SemaphoreType.DMA,
        ],
        compiler_params=pltpu.CompilerParams(collective_id=0, has_side_effects=True, vmem_limit_bytes=62 * 1024 * 1024),
        cost_estimate=pl.CostEstimate(flops=56 * 10 ** 9, bytes_accessed=330 * 10 ** 6, transcendentals=10 ** 7),
    )(x, ga, gm, cos, sin, *weights)[0]


def solution(mesh):
    act = P('fsdp', 'model', None)
    col = P(None, 'fsdp', 'model')
    row = P(None, 'model', 'fsdp')

    def device_step(x_in, gain_attn, gain_mlp, rope_cos, rope_sin, w_q, w_k, w_v, w_o, w_gate, w_up, w_down):
        def rows_of(t):
            return jnp.broadcast_to(t.reshape(8, 1, 8, TOK), (8, 8, 8, TOK)).reshape(ROWS, TOK)

        cos, sin = rows_of(rope_cos), rows_of(rope_sin)
        cos2 = jnp.concatenate([cos, cos], axis=1)
        sin2 = jnp.concatenate([-sin, sin], axis=1)
        def quarters(w):
            return w.reshape(w.shape[0], 2, 2, TOK, -1)

        def row_blocks(w):
            return w.reshape(w.shape[0], -1, 2, 2, TOK, UNIT)

        y = _call(x_in.reshape(TOK, 4096), gain_attn.reshape(2, 1, 4096), gain_mlp.reshape(2, 1, 4096), cos2, sin2,
                  quarters(w_q), quarters(w_k), quarters(w_v), row_blocks(w_o), quarters(w_gate), quarters(w_up), row_blocks(w_down))
        return y.reshape(x_in.shape)

    return jax.shard_map(device_step, mesh=mesh, in_specs=(act, P(), P(), P(), P(), col, col, col, row, col, col, row), out_specs=act, check_vma=False)
```

time: 1470 us -> 651 us (0.44)
  waiting for transfers between devices: 1270 us -> 0 us
  Pallas kernels: 0 us -> 642 us
  matrix products: 136 us -> 0 us
    all_gather x18 -> x0, waiting for transfers between devices: 1060 us -> none  [the longest x2 217 us: device_step(): wd_full = lax.all_gather(w_down[layer_idx], 'fsdp', axis=1, tiled=True)]
    pallas_call x0 -> x1, Pallas kernels: none -> 642 us  [_call(): pl.pallas_call(body, out_shape=(jax.ShapeDtypeStruct((TOK, 4096), bf), ja...]
    reduce_scatter x4 -> x0, waiting for transfers between devices: 207 us -> none  [the longest x2 105 us: device_step(): lax.psum_scatter(mlp_part, 'model', scatter_dimension=1, tiled=True)]
    dot_general x14 -> x0, matrix products: 136 us -> none  [the longest x2 62.6 us: device_step(): jnp.einsum('bsf,fd->bsd', hidden, wd_full, preferred_element_type=jnp.flo...]
  transfers between devices with their start and end apart: 22 -> 0, of which waited for: 22 -> 0; matrix products, arithmetic and copies ran while one was open for 6% -> 0% of each run, Pallas kernels for 0% -> 0%
where the time goes in v1:
time: 651 us; the launch traced here: 650 us
  Pallas kernels  642 us (99%)
    pallas_call x1, Pallas kernels, _call(): pl.pallas_call(body, out_shape=(jax.ShapeDtypeStruct((TOK, 4096), bf), ja...  642 us

profile of v1, /device:TPU:1, one launch (start us, length us, event | category | flops | bytes accessed | tf_op | source)
XLA Modules:
  0.0 649.7 jit_solution(4960312744321858082)
XLA Ops:
  0.0 1.4 reshape.44.ga_ref
  1.4 1.4 reshape.45.gm_ref
  2.8 0.8 broadcast_in_dim.15
  3.5 0.8 bitcast_negate_fusion
  4.3 0.8 broadcast_in_dim.17
  5.1 1.0 pad_maximum_fusion
  6.1 641.7 %shard_map.118 = (bf16[64,4096]{1,0:T(8,128)(2,1)}, bf16[52,16,2,2,64,256]{5,4,3,2,1,0:T(8,128)(2,1)}) custom-call(bf16[64,4096]{1,0:T(8,128)(2,1)} %bitcast.23, f32[2,1,4096]{2,1,0:T(1,128)} %reshape.44.ga_ref, f32[2,1,4096]{2,1,0:T(1,128)} %reshape.45.gm_ref, f32[512,128]{1,0:T(8,128)} %get-tuple-element.7.cos_ref, f32[512,128]{1,0:T(8,128)} %get-tuple-element.8.sin_ref, ...), custom_call_target="tpu_custom_call" | custom-call | flops 56000000000 | bytes 330000000 | tf_op jit(solution)/shard_map/pallas_call | solution.py:510
  647.8 1.9 copy.14

commit v2 on v0

v2 whole, which is shorter than its diff:
```python
import functools
import jax
import jax.numpy as jnp
from jax import lax
from jax.experimental import pallas as pl
from jax.experimental.pallas import tpu as pltpu
from jax.sharding import PartitionSpec as P

EPS = 1e-5
MESH = pl.DeviceIdType.MESH
FULL = slice(None)
RING = 4
FAR = 2
LANE = 128
UNIT = 256
ROWS = 512
TOK = 64
WIDE = 4096
HALF = 2048
HID = 896
DROW = 112
HEAD_SCALE = 128 ** -0.5
BOTH = (0, 1)
SIGNS = (1, -1)

N_AT, N_GU, N_DN = 5, 7, 4
KV, O_ITEM = 2, 3
PER_LAYER = N_AT + N_GU + N_DN
N_ITEMS = 2 * PER_LAYER
AHEAD = 2
SELF, NEXT, PAIR, OTHER = range(RING)


def _entry(stage, src, dst, sub, half, way):
    slot = [(v[0] % RING) * RING + v[1] % RING for v in (src, dst)]
    quarters = {(a, b) for a in BOTH for b in BOTH if sub in (a, None) and half in (b, None)}
    return dict(stage=stage, src=slot[0], dst=slot[1], sub=sub, half=half, way=way, q=quarters)


def _plan_all():
    plan = []
    for axis in BOTH:
        for sign in SIGNS:
            sub = (1 - sign) // 2

            def add(stage, along, across, sub, half):
                src = (along, across) if axis == 0 else (across, along)
                dst = (along - sign, across) if axis == 0 else (across, along - sign)
                plan.append(_entry(stage, src, dst, sub, half, (axis, sign)))

            add(0, 0, 0, None, None)
            add(1, -sign, 0, sub, None)
            for k in SIGNS:
                add(1, 0, k, None, axis)
                add(2, -sign, k, sub, axis)
            add(2, 0, FAR, None, axis)
            add(3, -sign, FAR, sub, axis)
    return plan


def _plan_half():
    plan = []

    def add(stage, dz, role, sub, half, way):
        if way in ("next", "pair"):
            to = {SELF: PAIR} if way == "pair" else {SELF: NEXT, PAIR: OTHER}
            dst = (dz, to[role])
        else:
            dst = (dz - way[1], role)
        plan.append(_entry(stage, (dz, role), dst, sub, half, way))

    add(0, 0, SELF, None, None, "pair")
    add(0, 0, SELF, None, None, "next")
    for sign in SIGNS:
        sub, way = (1 - sign) // 2, (0, sign)
        add(0, 0, SELF, None, None, way)
        add(1, -sign, SELF, sub, None, way)
        add(1, 0, NEXT, None, 0, way)
        add(1, 0, PAIR, None, None, way)
        add(2, -sign, NEXT, sub, 0, way)
        add(2, -sign, PAIR, sub, None, way)
        add(2, 0, OTHER, None, 0, way)
        add(3, -sign, OTHER, sub, 0, way)
        add(1, sign, SELF, None, 1, "next")
        add(2, sign, PAIR, None, 1, "next")
    add(1, 0, PAIR, None, None, "next")
    add(2, FAR, SELF, None, 1, "next")
    add(3, FAR, PAIR, None, 1, "next")
    return plan


ALL, SPLIT = _plan_all(), _plan_half()


def _of(plan, stage):
    return [i for i in range(len(plan)) if plan[i]["stage"] == stage]


def _cut(n, size):
    return FULL if n is None else pl.ds(n * size, size)


def body(x_ref, ga_ref, gm_ref, cos_ref, sin_ref, wq, wk, wv, wo, wg, wu, wd, y_ref, at_g, gu_g, dn_g,
         hu, wbuf, dbuf, part, t1, t2, t3, t4, zbuf, qbuf, kbuf, vbuf, obuf, res, acc,
         at_recv, gu_recv, dn_recv, at_send, gu_send, dn_send, ag_recv, ag_send, rs_recv, rs_send, pr_recv, pr_send, w_sem, d_sem):
    f_me = lax.axis_index("fsdp")
    m_me = lax.axis_index("model")
    z, y = lax.div(f_me, RING), lax.rem(f_me, RING)
    x, c = lax.div(m_me, 2), lax.rem(m_me, 2)
    up = lambda v: lax.rem(v + 1, RING)
    dn = lambda v: lax.rem(v + 3, RING)
    sib = 1 - c
    y_next = y + 1 - 2 * lax.rem(y, 2)
    side = lax.div(y, 2)

    dev_of = {"next": (z * RING + y_next, m_me), "pair": (z * RING + 3 - y, m_me)}
    for s, turn in zip(SIGNS, (up, dn)):
        dev_of[0, s] = (turn(z) * RING + y, m_me)
        dev_of[1, s] = (z * RING + turn(y), m_me)
    x_up, x_dn, x_far = up(x), dn(x), lax.rem(x + FAR, RING)
    dev_xu, dev_xd, dev_sib = (f_me, x_up * 2 + c), (f_me, x_dn * 2 + c), (f_me, x * 2 + sib)

    def lanes(n):
        return pl.ds(pl.multiple_of(n * LANE, LANE), LANE)

    def remote(src, dst, send, recv, dev):
        return pltpu.make_async_remote_copy(src_ref=src, dst_ref=dst, send_sem=send, recv_sem=recv, device_id=dev, device_id_type=MESH)

    kinds = {"at": (ALL, at_g, at_recv, at_send), "gu": (SPLIT, gu_g, gu_recv, gu_send), "dn": (SPLIT, dn_g, dn_recv, dn_send)}

    def stream_copy(kind, n, i):
        plan, g, recv, send = kinds[kind]
        p = plan[i]
        a, b = _cut(p["sub"], 1), _cut(p["half"], 1)
        at = p["src"] if p["stage"] else p["dst"]
        return remote(g.at[n, at, a, b], g.at[n, p["dst"], a, b], send.at[n], recv.at[n, i], dev_of[p["way"]])

    def own_unit(w, layer, j):
        return w.at[layer, :, :, :, pl.ds(pl.multiple_of(j * UNIT, UNIT), UNIT)]

    def own_gu(w, layer, j, h):
        return w.at[layer, :, :, :, lanes(h * N_GU + j)]

    def own_dn(layer, k, h):
        return wd.at[layer, h, lax.rem(k, 2), :, :, :, lanes(lax.div(k, 2))]

    def start_own(item):
        layer, pos = lax.div(item, PER_LAYER), lax.rem(item, PER_LAYER)

        def send(kind, n, src, lane=None):
            plan, g, recv, sems = kinds[kind]
            for i in _of(plan, 0):
                way = plan[i]["way"]
                dst = g.at[n, plan[i]["dst"]]
                if lane is not None:
                    dst = dst.at[:, :, :, pl.ds(lane, LANE)]
                remote(src(1 - side if way == "pair" else side), dst, sems.at[n], recv.at[n, i], dev_of[way]).start()

        @pl.when(pos < KV)
        def _():
            send("at", layer * N_AT + pos, lambda h: own_unit(wq, layer, pos))

        @pl.when(pos == KV)
        def _():
            for k, w in enumerate((wk, wv)):
                send("at", layer * N_AT + pos, lambda h: w.at[layer], k * LANE)

        @pl.when(jnp.logical_and(pos >= O_ITEM, pos < N_AT))
        def _():
            send("at", layer * N_AT + pos, lambda h: wo.at[layer, pos - O_ITEM])

        @pl.when(jnp.logical_and(pos >= N_AT, pos < N_AT + N_GU))
        def _():
            j = pos - N_AT
            for k, w in enumerate((wg, wu)):
                send("gu", layer * N_GU + j, lambda h: own_gu(w, layer, j, h), k * LANE)

        @pl.when(pos >= N_AT + N_GU)
        def _():
            k = pos - N_AT - N_GU
            send("dn", layer * N_DN + k, lambda h: own_dn(layer, k, h))

    def serve(kind, n, stage):
        plan = kinds[kind][0]
        waited = set()
        before = _of(plan, stage - 1)
        for i in _of(plan, stage):
            for j in before:
                if j not in waited and plan[j]["dst"] == plan[i]["src"] and plan[j]["q"] & plan[i]["q"]:
                    stream_copy(kind, n, j).wait_recv()
                    waited.add(j)
            stream_copy(kind, n, i).start()
        for j in before:
            if j not in waited:
                stream_copy(kind, n, j).wait_recv()

    def forward(item, stage):
        layer, pos = lax.div(item, PER_LAYER), lax.rem(item, PER_LAYER)

        @pl.when(pos < N_AT)
        def _():
            serve("at", layer * N_AT + pos, stage)

        @pl.when(jnp.logical_and(pos >= N_AT, pos < N_AT + N_GU))
        def _():
            serve("gu", layer * N_GU + pos - N_AT, stage)

        @pl.when(pos >= N_AT + N_GU)
        def _():
            serve("dn", layer * N_DN + pos - N_AT - N_GU, stage)

    def tick(t):
        for lag in range(RING):
            @pl.when(jnp.logical_and(t >= lag, t < N_ITEMS + lag))
            def _():
                forward(t - lag, lag + 1)

            if lag == FAR:
                @pl.when(t + AHEAD < N_ITEMS)
                def _():
                    start_own(t + AHEAD)

    def ag_copy(inst, k):
        slot = lax.rem(inst, 3)
        own, lo, hi, far = (x * 2 + c), (x_dn * 2 + c), (x_up * 2 + c), (x_far * 2 + c)
        s0, s1 = _cut(0, TOK // 2), _cut(1, TOK // 2)
        blk, rows, dev = [
            (own, FULL, dev_sib), (own, FULL, dev_xu), (own, FULL, dev_xd),
            (lo, s0, dev_xu), (hi, s1, dev_xd),
            (lo, FULL, dev_sib), (hi, FULL, dev_sib), (far, FULL, dev_sib)][k]
        ref = hu.at[slot, blk, rows]
        return remote(ref, ref, ag_send.at[inst, k], ag_recv.at[inst, k], dev)

    def ag_start(inst):
        for k in (1, 2, 0):
            ag_copy(inst, k).start()

    def ag_mid(inst):
        for a, b, d in ((1, 3, 5), (2, 4, 6)):
            ag_copy(inst, a).wait_recv()
            ag_copy(inst, b).start()
            ag_copy(inst, d).start()

    def ag_end(inst):
        for k in (3, 4):
            ag_copy(inst, k).wait_recv()
        ag_copy(inst, 7).start()
        for k in (0, 5, 6, 7):
            ag_copy(inst, k).wait_recv()
        for k in range(8):
            ag_copy(inst, k).wait_send()

    def pair_copy(layer, k):
        if k == 0:
            src, dst = hu.at[1, m_me], hu.at[2, m_me]
        else:
            src, dst = part.at[k - 1, 1, x, c], t4.at[k - 1]
        return remote(src, dst, pr_send.at[layer, k], pr_recv.at[layer, k], dev_of["pair"])

    def rs_copy(inst, hh, k, groups):
        g = pl.ds(0, groups)
        lo, hi = _cut(0, TOK // 2), _cut(1, TOK // 2)
        src, dst, dev = [
            (part.at[hh, g, :, sib], t1.at[hh, g], dev_sib),
            (part.at[hh, g, x_far, c, lo], t2.at[hh, g, 0], dev_xu),
            (part.at[hh, g, x_far, c, hi], t2.at[hh, g, 1], dev_xd),
            (part.at[hh, g, x_up, c], t3.at[hh, g, 0], dev_xu),
            (part.at[hh, g, x_dn, c], t3.at[hh, g, 1], dev_xd)][k]
        return remote(src, dst, rs_send.at[inst, hh, k], rs_recv.at[inst, hh, k], dev)

    def rs_core(inst, hh, groups):
        rs_copy(inst, hh, 0, groups).start()

    def rs_far(inst, hh, groups):
        rs_copy(inst, hh, 0, groups).wait_recv()

        def add(xp):
            def one(g, _):
                part[hh, g, xp, c] = part[hh, g, xp, c] + t1[hh, g, xp]
                return 0
            lax.fori_loop(0, groups, one, 0)

        add(x_far)
        for k in (1, 2):
            rs_copy(inst, hh, k, groups).start()
        for xp in (x_up, x_dn, x):
            add(xp)

    def rs_near(inst, hh, groups):
        for b, xp in ((0, x_up), (1, x_dn)):
            rs_copy(inst, hh, 1 + b, groups).wait_recv()
            r = _cut(b, TOK // 2)
            for g in range(groups):
                part[hh, g, xp, c, r] = part[hh, g, xp, c, r] + t2[hh, g, b]
            rs_copy(inst, hh, 3 + b, groups).start()

    def rs_wait(inst, hh, groups):
        for k in (3, 4):
            rs_copy(inst, hh, k, groups).wait_recv()
        for k in range(5):
            rs_copy(inst, hh, k, groups).wait_send()

    def pair_out(layer, hh):
        rs_wait(2 * layer + 1, hh, 2)
        part[hh, 1, x, c] = part[hh, 1, x, c] + t3[hh, 1, 0] + t3[hh, 1, 1]
        pair_copy(layer, hh + 1).start()

    def pair_in(layer, hh):
        pair_copy(layer, hh + 1).wait()

    def rows16(i):
        return pl.ds(pl.multiple_of(i * 16, 16), 16)

    def add_residual(paired):
        def step(i, _):
            r = rows16(i)
            s = [part[hh, 0, x, c, r] + t3[hh, 0, 0, r] + t3[hh, 0, 1, r] for hh in BOTH]
            if paired:
                s = [s[hh] + t4[hh, r] for hh in BOTH]
            cols = [s[hh][:, f * LANE:(f + 1) * LANE] for f in range(16) for hh in BOTH]
            res[r] = (res[r].astype(jnp.float32) + jnp.concatenate(cols, axis=1)).astype(jnp.bfloat16)
            return 0
        lax.fori_loop(0, RING, step, 0)

    def norm_into(slot, gain):
        def step(i, _):
            r = rows16(i)
            v = res[r].astype(jnp.float32)
            ms = jnp.mean(v * v, axis=-1, keepdims=True)
            hu[slot, m_me, r] = (v * lax.rsqrt(ms + EPS) * gain).astype(jnp.bfloat16)
            return 0
        lax.fori_loop(0, RING, step, 0)

    def src_all(rel):
        return lax.rem(z + lax.div(rel, RING), RING) * RING + lax.rem(y + lax.rem(rel, RING), RING)

    def src_split(rel):
        role = lax.rem(rel, RING)
        b = y + lax.rem(role, 2) * (y_next - y)
        return lax.rem(z + lax.div(rel, RING), RING) * RING + b + lax.div(role, 2) * (3 - 2 * b)

    def load_unit(g, n, slot, own, where):
        mine = wbuf.at[slot, f_me]
        if len(own) == 1:
            pltpu.make_async_copy(own[0], mine, w_sem.at[slot]).start()
        else:
            for k in BOTH:
                pltpu.make_async_copy(own[k], mine.at[:, :, :, pl.ds(k * LANE, LANE)], w_sem.at[slot]).start()

        def one(rel, _):
            pltpu.make_async_copy(g.at[n, rel], wbuf.at[slot, where(rel)], w_sem.at[slot]).start()
            return 0
        lax.fori_loop(1, 16, one, 0)

    def wait_unit(slot):
        pltpu.make_async_copy(wbuf.at[slot], wbuf.at[slot], w_sem.at[slot]).wait()

    def load_down(layer, hh):
        for r in BOTH:
            k = 2 * hh + r
            pltpu.make_async_copy(own_dn(layer, k, side), dbuf.at[r, :, :, :, lanes(f_me)], d_sem).start()

            def one(rel, _):
                pltpu.make_async_copy(dn_g.at[layer * N_DN + k, rel], dbuf.at[r, :, :, :, lanes(src_split(rel))], d_sem).start()
                return 0
            lax.fori_loop(1, 16, one, 0)

    def project(slot, ws):
        acc[...] = jnp.zeros_like(acc)

        def step(kk, _):
            lhs = hu[slot, :, :, pl.ds(pl.multiple_of(kk * ROWS, ROWS), ROWS)].reshape(ROWS, ROWS)
            rhs = wbuf[ws, pl.ds(2 * kk, 2)].reshape(ROWS, UNIT)
            acc[...] += jnp.dot(lhs, rhs, preferred_element_type=jnp.float32)
            return 0
        lax.fori_loop(0, 8, step, 0)

    def rows128(i):
        return pl.ds(pl.multiple_of(i * LANE, LANE), LANE)

    def rope_store(lane, dst):
        def step(i, _):
            r = rows128(i)
            v = acc[r, lane:lane + LANE].astype(jnp.bfloat16).astype(jnp.float32)
            dst[r] = (v * cos_ref[r] + pltpu.roll(v, TOK, 1) * sin_ref[r]).astype(jnp.bfloat16)
            return 0
        lax.fori_loop(0, RING, step, 0)

    def qkv(layer):
        base = layer * N_AT
        for u in BOTH:
            load_unit(at_g, base + u, u, [own_unit(wq, layer, u)], src_all)
        load_unit(at_g, base + KV, KV, [wk.at[layer], wv.at[layer]], src_all)
        for u in BOTH:
            wait_unit(u)
            project(0, u)
            for h in BOTH:
                rope_store(h * LANE, qbuf.at[2 * u + h])
        wait_unit(KV)
        project(0, KV)
        rope_store(0, kbuf)
        vbuf[...] = acc[:, LANE:].astype(jnp.bfloat16)
        for u in BOTH:
            load_unit(at_g, base + O_ITEM + u, u, [wo.at[layer, u]], src_all)

    def attention():
        def step(i, _):
            r = rows128(i)
            qi = lax.broadcasted_iota(jnp.int32, (LANE, ROWS), 0) + i * LANE
            ki = lax.broadcasted_iota(jnp.int32, (LANE, ROWS), 1)
            same = ((qi >> 3) & 7) == ((ki >> 3) & 7)
            qpos = (qi >> 6) * 8 + (qi & 7)
            kpos = (ki >> 6) * 8 + (ki & 7)
            ok = jnp.logical_and(same, qpos >= kpos)
            for h in range(RING):
                s = lax.dot_general(qbuf[h, r], kbuf[...], (((1,), (1,)), ((), ())), preferred_element_type=jnp.float32)
                s = jnp.where(ok, s * HEAD_SCALE, -jnp.inf)
                e = jnp.exp(s - jnp.max(s, axis=-1, keepdims=True))
                p = (e / jnp.sum(e, axis=-1, keepdims=True)).astype(jnp.bfloat16)
                o = jnp.dot(p, vbuf[...], preferred_element_type=jnp.float32)
                obuf[r, h * LANE:(h + 1) * LANE] = o.astype(jnp.bfloat16)
            return 0
        lax.fori_loop(0, RING, step, 0)

    def out_proj():
        for u in BOTH:
            wait_unit(u)

        def step(f, _):
            out = sum(jnp.dot(obuf[:, u * UNIT:(u + 1) * UNIT], wbuf[u, f].reshape(UNIT, UNIT), preferred_element_type=jnp.float32) for u in BOTH)
            for hh in BOTH:
                part[hh, 0, :, :, :, lanes(f)] = out[:, hh * LANE:(hh + 1) * LANE].reshape(RING, 2, TOK, LANE)
            return 0
        lax.fori_loop(0, 16, step, 0)

    def gate_up(layer, group):
        def load(j):
            load_unit(gu_g, layer * N_GU + j, lax.rem(j, 2), [own_gu(wg, layer, j, side), own_gu(wu, layer, j, side)], src_split)

        load(0)

        def step(j, _):
            @pl.when(j + 1 < N_GU)
            def _():
                load(j + 1)
            wait_unit(lax.rem(j, 2))
            project(1 + group, lax.rem(j, 2))

            def rows(i, _):
                r = rows128(i)
                hid = jax.nn.silu(acc[r, 0:LANE]) * acc[r, LANE:]
                zbuf[group, r, lanes(j)] = hid.astype(jnp.bfloat16)
                return 0
            lax.fori_loop(0, RING, rows, 0)
            return 0
        lax.fori_loop(0, N_GU, step, 0)

    def down(layer, hh):
        load_down(layer, hh)
        pltpu.make_async_copy(dbuf, dbuf, d_sem).wait()

        def tile(n, _):
            cols = pl.ds(pl.multiple_of(n * UNIT, UNIT), UNIT)
            rhs = dbuf[:, :, :, :, cols].reshape(HID, UNIT)
            for g in BOTH:
                out = jnp.dot(zbuf[g], rhs, preferred_element_type=jnp.float32)
                part[hh, g, :, :, :, cols] = out.reshape(RING, 2, TOK, UNIT)
            return 0
        lax.fori_loop(0, 8, tile, 0)

    barrier = pltpu.get_barrier_semaphore()
    peers = [dev_of[a, s] for a in BOTH for s in SIGNS] + [dev_xu, dev_xd, dev_sib]
    for dev in peers:
        pl.semaphore_signal(barrier, inc=1, device_id=dev, device_id_type=MESH)
    pl.semaphore_wait(barrier, len(peers))

    for item in range(AHEAD):
        start_own(item)
    res[...] = x_ref[...]
    norm_into(0, ga_ref[0])
    ag_start(0)

    def next_layer(layer):
        @pl.when(layer == 0)
        def _():
            norm_into(0, ga_ref[1])
            ag_start(3)

    def each(fn, *args):
        for hh in BOTH:
            fn(args[0], hh, *args[1:])

    hooks = [
        (23, 40, lambda l: (each(pair_in, l), add_residual(True), next_layer(l))),
        (5, 24, lambda l: ag_mid(3 * l)),
        (7, 25, lambda l: (ag_end(3 * l), qkv(l))),
        (8, 25, lambda l: attention()),
        (8, 26, lambda l: (out_proj(), each(rs_core, 2 * l, 1))),
        (9, 26, lambda l: each(rs_far, 2 * l, 1)),
        (10, 27, lambda l: each(rs_near, 2 * l, 1)),
        (11, 28, lambda l: (each(rs_wait, 2 * l, 1), add_residual(False), norm_into(1, gm_ref[l]), pair_copy(l, 0).start(), ag_start(3 * l + 1))),
        (12, 29, lambda l: ag_mid(3 * l + 1)),
        (13, 30, lambda l: (pair_copy(l, 0).wait(), ag_start(3 * l + 2), ag_end(3 * l + 1))),
        (14, 31, lambda l: gate_up(l, 0)),
        (15, 31, lambda l: ag_mid(3 * l + 2)),
        (16, 32, lambda l: (ag_end(3 * l + 2), gate_up(l, 1))),
        (17, 33, lambda l: (down(l, 0), rs_core(2 * l + 1, 0, 2))),
        (18, 35, lambda l: (down(l, 1), rs_core(2 * l + 1, 1, 2), rs_far(2 * l + 1, 0, 2))),
        (19, 36, lambda l: rs_far(2 * l + 1, 1, 2)),
        (20, 37, lambda l: rs_near(2 * l + 1, 0, 2)),
        (21, 38, lambda l: (rs_near(2 * l + 1, 1, 2), pair_out(l, 0))),
        (22, 39, lambda l: pair_out(l, 1)),
    ]

    def step(t, _):
        tick(t)
        for t0, t1_, what in hooks:
            @pl.when(jnp.logical_or(t == t0, t == t1_))
            def _():
                what(jnp.where(t == t1_, 1, 0))
        return 0
    lax.fori_loop(0, 41, step, 0)
    y_ref[...] = res[...]

    for plan, g, _, send in kinds.values():
        def drain(n, _):
            span = g.at[n, pl.ds(0, 15)]
            pltpu.make_async_copy(span, span, send.at[n]).wait()
            return 0
        lax.fori_loop(0, g.shape[0], drain, 0)


def _call(x, ga, gm, cos, sin, *weights):
    bf, f32 = jnp.bfloat16, jnp.float32
    vm = pl.BlockSpec(memory_space=pltpu.VMEM)
    anys = pl.BlockSpec(memory_space=pl.ANY)
    dma = pltpu.SemaphoreType.DMA
    n_at, n_gu, n_dn = 2 * N_AT, 2 * N_GU, 2 * N_DN
    unit = (16, 2, 2, TOK, UNIT)
    return pl.pallas_call(
        body,
        out_shape=(jax.ShapeDtypeStruct((TOK, WIDE), bf), jax.ShapeDtypeStruct((n_at, *unit), bf),
                   jax.ShapeDtypeStruct((n_gu, *unit), bf), jax.ShapeDtypeStruct((n_dn, 16, 2, 2, DROW, LANE), bf)),
        in_specs=[vm] * 5 + [anys] * len(weights),
        out_specs=(vm, anys, anys, anys),
        scratch_shapes=[
            pltpu.VMEM((3, 8, TOK, WIDE), bf),
            pltpu.VMEM((3, *unit), bf),
            pltpu.VMEM((2, 2, 2, DROW, HALF), bf),
            pltpu.VMEM((2, 2, RING, 2, TOK, HALF), f32),
            pltpu.VMEM((2, 2, RING, TOK, HALF), f32),
            pltpu.VMEM((2, 2, 2, TOK // 2, HALF), f32),
            pltpu.VMEM((2, 2, 2, TOK, HALF), f32),
            pltpu.VMEM((2, TOK, HALF), f32),
            pltpu.VMEM((2, ROWS, HID), bf),
            pltpu.VMEM((RING, ROWS, LANE), bf),
            pltpu.VMEM((ROWS, LANE), bf),
            pltpu.VMEM((ROWS, LANE), bf),
            pltpu.VMEM((ROWS, ROWS), bf),
            pltpu.VMEM((TOK, WIDE), bf),
            pltpu.VMEM((ROWS, UNIT), f32),
            dma((n_at, len(ALL))), dma((n_gu, len(SPLIT))), dma((n_dn, len(SPLIT))),
            dma((n_at,)), dma((n_gu,)), dma((n_dn,)),
            dma((6, 8)), dma((6, 8)), dma((RING, 2, 5)), dma((RING, 2, 5)), dma((2, 3)), dma((2, 3)), dma((3,)), dma,
        ],
        compiler_params=pltpu.CompilerParams(collective_id=0, has_side_effects=True, vmem_limit_bytes=63 * 1024 * 1024),
        cost_estimate=pl.CostEstimate(flops=56 * 10 ** 9, bytes_accessed=330 * 10 ** 6, transcendentals=10 ** 7),
    )(x, ga, gm, cos, sin, *weights)[0]


def solution(mesh):
    act = P('fsdp', 'model', None)
    col = P(None, 'fsdp', 'model')
    row = P(None, 'model', 'fsdp')

    def device_step(x_in, gain_attn, gain_mlp, rope_cos, rope_sin, w_q, w_k, w_v, w_o, w_gate, w_up, w_down):
        def rows_of(t):
            return jnp.broadcast_to(t.reshape(8, 1, 8, TOK), (8, 8, 8, TOK)).reshape(ROWS, TOK)

        cos, sin = rows_of(rope_cos), rows_of(rope_sin)
        cos2 = jnp.concatenate([cos, cos], axis=1)
        sin2 = jnp.concatenate([-sin, sin], axis=1)
        def quarters(w):
            return w.reshape(w.shape[0], 2, 2, TOK, -1)


        y = _call(x_in.reshape(TOK, 4096), gain_attn.reshape(2, 1, 4096), gain_mlp.reshape(2, 1, 4096), cos2, sin2,
                  quarters(w_q), quarters(w_k), quarters(w_v), w_o.reshape(2, 2, 2, 2, TOK, UNIT), quarters(w_gate), quarters(w_up), w_down.reshape(2, 2, 2, 2, 2, DROW, UNIT))
        return y.reshape(x_in.shape)

    return jax.shard_map(device_step, mesh=mesh, in_specs=(act, P(), P(), P(), P(), col, col, col, row, col, col, row), out_specs=act, check_vma=False)
```

time: 1470 us -> 619 us (0.42)
  waiting for transfers between devices: 1270 us -> 0 us
  Pallas kernels: 0 us -> 610 us
  matrix products: 136 us -> 0 us
    all_gather x18 -> x0, waiting for transfers between devices: 1060 us -> none  [the longest x2 217 us: device_step(): wd_full = lax.all_gather(w_down[layer_idx], 'fsdp', axis=1, tiled=True)]
    pallas_call x0 -> x1, Pallas kernels: none -> 610 us  [_call(): pl.pallas_call(body, out_shape=(jax.ShapeDtypeStruct((TOK, WIDE), bf), ja...]
    reduce_scatter x4 -> x0, waiting for transfers between devices: 207 us -> none  [the longest x2 105 us: device_step(): lax.psum_scatter(mlp_part, 'model', scatter_dimension=1, tiled=True)]
    dot_general x14 -> x0, matrix products: 136 us -> none  [the longest x2 62.6 us: device_step(): jnp.einsum('bsf,fd->bsd', hidden, wd_full, preferred_element_type=jnp.flo...]
  transfers between devices with their start and end apart: 22 -> 0, of which waited for: 22 -> 0; matrix products, arithmetic and copies ran while one was open for 6% -> 0% of each run, Pallas kernels for 0% -> 0%
where the time goes in v2:
time: 619 us; the launch traced here: 618 us
  Pallas kernels  610 us (99%)
    pallas_call x1, Pallas kernels, _call(): pl.pallas_call(body, out_shape=(jax.ShapeDtypeStruct((TOK, WIDE), bf), ja...  610 us

profile of v2, /device:TPU:1, one launch (start us, length us, event | category | flops | bytes accessed | tf_op | source)
XLA Modules:
  0.0 618.1 jit_solution(6771615435730313381)
XLA Ops:
  0.0 1.4 reshape.44.ga_ref
  1.4 1.4 reshape.45.gm_ref
  2.8 0.8 broadcast_in_dim.15
  3.5 0.8 bitcast_negate_fusion
  4.3 0.8 broadcast_in_dim.17
  5.1 1.0 pad_maximum_fusion
  6.1 610.1 %shard_map.118 = (bf16[64,4096]{1,0:T(8,128)(2,1)}, bf16[10,16,2,2,64,256]{5,4,3,2,1,0:T(8,128)(2,1)}, bf16[14,16,2,2,64,256]{5,4,3,2,1,0:T(8,128)(2,1)}, bf16[8,16,2,2,112,128]{5,4,3,2,1,0:T(8,128)(2,1)}) custom-call(bf16[64,4096]{1,0:T(8,128)(2,1)} %bitcast.23, f32[2,1,4096]{2,1,0:T(1,128)} %reshape.44.ga_ref, f32[2,1,4096]{2,1,0:T(1,128)} %reshape.45.gm_ref, ...), custom_call_target="tpu_custom_call" | custom-call | flops 56000000000 | bytes 330000000 | tf_op jit(solution)/shard_map/pallas_call | solution.py:540
  616.2 1.9 copy.14

commit v3 on v2

v3 whole, which is shorter than its diff:
```python
import functools
import jax
import jax.numpy as jnp
from jax import lax
from jax.experimental import pallas as pl
from jax.experimental.pallas import tpu as pltpu
from jax.sharding import PartitionSpec as P

EPS = 1e-5
MESH = pl.DeviceIdType.MESH
FULL = slice(None)
RING = 4
FAR = 2
LANE = 128
UNIT = 256
ROWS = 512
TOK = 64
WIDE = 4096
HALF = 2048
SUB = 32
GRP = 256
HID = 896
DROW = 112
HEAD_SCALE = 128 ** -0.5
BOTH = (0, 1)
SIGNS = (1, -1)

N_AT, N_GU, N_DN = 5, 7, 4
KV, O_ITEM = 2, 3
PER_LAYER = N_AT + N_GU + N_DN
N_ITEMS = 2 * PER_LAYER
AHEAD = 2
SELF, NEXT, PAIR, OTHER = range(RING)


def _entry(stage, src, dst, sub, half, way):
    slot = [(v[0] % RING) * RING + v[1] % RING for v in (src, dst)]
    quarters = {(a, b) for a in BOTH for b in BOTH if sub in (a, None) and half in (b, None)}
    return dict(stage=stage, src=slot[0], dst=slot[1], sub=sub, half=half, way=way, q=quarters)


def _plan_all():
    plan = []
    for axis in BOTH:
        for sign in SIGNS:
            sub = (1 - sign) // 2

            def add(stage, along, across, sub, half):
                src = (along, across) if axis == 0 else (across, along)
                dst = (along - sign, across) if axis == 0 else (across, along - sign)
                plan.append(_entry(stage, src, dst, sub, half, (axis, sign)))

            add(0, 0, 0, None, None)
            add(1, -sign, 0, sub, None)
            for k in SIGNS:
                add(1, 0, k, None, axis)
                add(2, -sign, k, sub, axis)
            add(2, 0, FAR, None, axis)
            add(3, -sign, FAR, sub, axis)
    return plan


def _plan_half():
    plan = []

    def add(stage, dz, role, sub, half, way):
        if way in ("next", "pair"):
            to = {SELF: PAIR} if way == "pair" else {SELF: NEXT, PAIR: OTHER}
            dst = (dz, to[role])
        else:
            dst = (dz - way[1], role)
        plan.append(_entry(stage, (dz, role), dst, sub, half, way))

    add(0, 0, SELF, None, None, "pair")
    add(0, 0, SELF, None, None, "next")
    for sign in SIGNS:
        sub, way = (1 - sign) // 2, (0, sign)
        add(0, 0, SELF, None, None, way)
        add(1, -sign, SELF, sub, None, way)
        add(1, 0, NEXT, None, 0, way)
        add(1, 0, PAIR, None, None, way)
        add(2, -sign, NEXT, sub, 0, way)
        add(2, -sign, PAIR, sub, None, way)
        add(2, 0, OTHER, None, 0, way)
        add(3, -sign, OTHER, sub, 0, way)
        add(1, sign, SELF, None, 1, "next")
        add(2, sign, PAIR, None, 1, "next")
    add(1, 0, PAIR, None, None, "next")
    add(2, FAR, SELF, None, 1, "next")
    add(3, FAR, PAIR, None, 1, "next")
    return plan


ALL, SPLIT = _plan_all(), _plan_half()


def _of(plan, stage):
    return [i for i in range(len(plan)) if plan[i]["stage"] == stage]


def _cut(n, size):
    return FULL if n is None else pl.ds(n * size, size)


def body(x_ref, ga_ref, gm_ref, cos_ref, sin_ref, wq, wk, wv, wo, wg, wu, wd, y_ref, at_g, gu_g, dn_g,
         hu, wbuf, dbuf, part, t1, t2, t3, t4, zbuf, qbuf, kbuf, vbuf, obuf, res, acc,
         at_recv, gu_recv, dn_recv, at_send, gu_send, dn_send, ag_recv, ag_send, rs_recv, rs_send, pr_recv, pr_send, w_sem, d_sem):
    f_me = lax.axis_index("fsdp")
    m_me = lax.axis_index("model")
    z, y = lax.div(f_me, RING), lax.rem(f_me, RING)
    x, c = lax.div(m_me, 2), lax.rem(m_me, 2)
    up = lambda v: lax.rem(v + 1, RING)
    dn = lambda v: lax.rem(v + 3, RING)
    sib = 1 - c
    y_next = y + 1 - 2 * lax.rem(y, 2)
    side = lax.div(y, 2)

    dev_of = {"next": (z * RING + y_next, m_me), "pair": (z * RING + 3 - y, m_me)}
    for s, turn in zip(SIGNS, (up, dn)):
        dev_of[0, s] = (turn(z) * RING + y, m_me)
        dev_of[1, s] = (z * RING + turn(y), m_me)
    x_up, x_dn, x_far = up(x), dn(x), lax.rem(x + FAR, RING)
    dev_xu, dev_xd, dev_sib = (f_me, x_up * 2 + c), (f_me, x_dn * 2 + c), (f_me, x * 2 + sib)

    def lanes(n):
        return pl.ds(pl.multiple_of(n * LANE, LANE), LANE)

    def remote(src, dst, send, recv, dev):
        return pltpu.make_async_remote_copy(src_ref=src, dst_ref=dst, send_sem=send, recv_sem=recv, device_id=dev, device_id_type=MESH)

    kinds = {"at": (ALL, at_g, at_recv, at_send), "gu": (SPLIT, gu_g, gu_recv, gu_send), "dn": (SPLIT, dn_g, dn_recv, dn_send)}

    def stream_copy(kind, n, i):
        plan, g, recv, send = kinds[kind]
        p = plan[i]
        a, b = _cut(p["sub"], 1), _cut(p["half"], 1)
        at = p["src"] if p["stage"] else p["dst"]
        return remote(g.at[n, at, a, b], g.at[n, p["dst"], a, b], send.at[n], recv.at[n, i], dev_of[p["way"]])

    def own_unit(w, layer, j):
        return w.at[layer, :, :, :, pl.ds(pl.multiple_of(j * UNIT, UNIT), UNIT)]

    def own_gu(w, layer, j, h):
        return w.at[layer, :, :, :, lanes(h * N_GU + j)]

    def own_dn(layer, k, h):
        return wd.at[layer, h, lax.rem(k, 2), :, :, :, lanes(lax.div(k, 2))]

    def start_own(item):
        layer, pos = lax.div(item, PER_LAYER), lax.rem(item, PER_LAYER)

        def send(kind, n, src, lane=None):
            plan, g, recv, sems = kinds[kind]
            for i in _of(plan, 0):
                way = plan[i]["way"]
                dst = g.at[n, plan[i]["dst"]]
                if lane is not None:
                    dst = dst.at[:, :, :, pl.ds(lane, LANE)]
                remote(src(1 - side if way == "pair" else side), dst, sems.at[n], recv.at[n, i], dev_of[way]).start()

        @pl.when(pos < KV)
        def _():
            send("at", layer * N_AT + pos, lambda h: own_unit(wq, layer, pos))

        @pl.when(pos == KV)
        def _():
            for k, w in enumerate((wk, wv)):
                send("at", layer * N_AT + pos, lambda h: w.at[layer], k * LANE)

        @pl.when(jnp.logical_and(pos >= O_ITEM, pos < N_AT))
        def _():
            send("at", layer * N_AT + pos, lambda h: wo.at[layer, pos - O_ITEM])

        @pl.when(jnp.logical_and(pos >= N_AT, pos < N_AT + N_GU))
        def _():
            j = pos - N_AT
            for k, w in enumerate((wg, wu)):
                send("gu", layer * N_GU + j, lambda h: own_gu(w, layer, j, h), k * LANE)

        @pl.when(pos >= N_AT + N_GU)
        def _():
            k = pos - N_AT - N_GU
            send("dn", layer * N_DN + k, lambda h: own_dn(layer, k, h))

    def serve(kind, n, stage):
        plan = kinds[kind][0]
        waited = set()
        before = _of(plan, stage - 1)
        for i in _of(plan, stage):
            for j in before:
                if j not in waited and plan[j]["dst"] == plan[i]["src"] and plan[j]["q"] & plan[i]["q"]:
                    stream_copy(kind, n, j).wait_recv()
                    waited.add(j)
            stream_copy(kind, n, i).start()
        for j in before:
            if j not in waited:
                stream_copy(kind, n, j).wait_recv()

    def forward(item, stage):
        layer, pos = lax.div(item, PER_LAYER), lax.rem(item, PER_LAYER)

        @pl.when(pos < N_AT)
        def _():
            serve("at", layer * N_AT + pos, stage)

        @pl.when(jnp.logical_and(pos >= N_AT, pos < N_AT + N_GU))
        def _():
            serve("gu", layer * N_GU + pos - N_AT, stage)

        @pl.when(pos >= N_AT + N_GU)
        def _():
            serve("dn", layer * N_DN + pos - N_AT - N_GU, stage)

    def tick(u):
        t = lax.div(u, RING)
        for lag in range(RING):
            @pl.when(jnp.logical_and(lax.rem(u, RING) == lag, jnp.logical_and(t >= N_AT + lag, t < N_ITEMS + lag)))
            def _():
                forward(t - lag, lag + 1)

        @pl.when(jnp.logical_and(lax.rem(u, RING) == FAR, t + AHEAD < N_ITEMS))
        def _():
            start_own(t + AHEAD)

    def ag_copy(layer, slot, th, k):
        own, lo, hi, far = (x * 2 + c), (x_dn * 2 + c), (x_up * 2 + c), (x_far * 2 + c)
        s0, s1 = _cut(0, SUB // 2), _cut(1, SUB // 2)
        blk, rows, dev = [
            (own, FULL, dev_sib), (own, FULL, dev_xu), (own, FULL, dev_xd),
            (lo, s0, dev_xu), (hi, s1, dev_xd),
            (lo, FULL, dev_sib), (hi, FULL, dev_sib), (far, FULL, dev_sib)][k]
        ref = hu.at[th, slot, blk, rows]
        return remote(ref, ref, ag_send.at[layer, slot, th, k], ag_recv.at[layer, slot, th, k], dev)

    def ag_start(*inst):
        for k in (1, 2, 0):
            ag_copy(*inst, k).start()

    def ag_mid(*inst):
        for a, b, d in ((1, 3, 5), (2, 4, 6)):
            ag_copy(*inst, a).wait_recv()
            ag_copy(*inst, b).start()
            ag_copy(*inst, d).start()

    def ag_end(*inst):
        for k in (3, 4):
            ag_copy(*inst, k).wait_recv()
        ag_copy(*inst, 7).start()
        for k in (0, 5, 6, 7):
            ag_copy(*inst, k).wait_recv()
        for k in range(8):
            ag_copy(*inst, k).wait_send()

    def pair_tokens(layer, th):
        return remote(hu.at[th, 1, m_me], hu.at[th, 2, m_me], pr_send.at[layer, th, 2], pr_recv.at[layer, th, 2], dev_of["pair"])

    def pair_sums(layer, th, hh):
        return remote(part.at[th, hh, 1, x, c], t4.at[th, hh], pr_send.at[layer, th, hh], pr_recv.at[layer, th, hh], dev_of["pair"])

    def spans(kind):
        return (BOTH, (0,)) if kind == 2 else ((kind,), BOTH)

    def rs_copy(layer, kind, th, k):
        hs, gs = spans(kind)
        h, g = pl.ds(hs[0], len(hs)), pl.ds(0, len(gs))
        lo, hi = _cut(0, SUB // 2), _cut(1, SUB // 2)
        src, dst, dev = [
            (part.at[th, h, g, :, sib], t1.at[th, h, g], dev_sib),
            (part.at[th, h, g, x_far, c, lo], t2.at[th, h, g, 0], dev_xu),
            (part.at[th, h, g, x_far, c, hi], t2.at[th, h, g, 1], dev_xd),
            (part.at[th, h, g, x_up, c], t3.at[th, h, g, 0], dev_xu),
            (part.at[th, h, g, x_dn, c], t3.at[th, h, g, 1], dev_xd)][k]
        return remote(src, dst, rs_send.at[layer, kind, th, k], rs_recv.at[layer, kind, th, k], dev)

    def rs_far(layer, kind, th):
        rs_copy(layer, kind, th, 0).wait_recv()

        def add(xp):
            for h in spans(kind)[0]:
                for g in spans(kind)[1]:
                    part[th, h, g, xp, c] = part[th, h, g, xp, c] + t1[th, h, g, xp]

        add(x_far)
        for k in (1, 2):
            rs_copy(layer, kind, th, k).start()
        for xp in (x_up, x_dn, x):
            add(xp)

    def rs_near(layer, kind, th):
        for b, xp in ((0, x_up), (1, x_dn)):
            rs_copy(layer, kind, th, 1 + b).wait_recv()
            r = _cut(b, SUB // 2)
            for h in spans(kind)[0]:
                for g in spans(kind)[1]:
                    part[th, h, g, xp, c, r] = part[th, h, g, xp, c, r] + t2[th, h, g, b]
            rs_copy(layer, kind, th, 3 + b).start()

    def rs_wait(layer, kind, th):
        for k in (3, 4):
            rs_copy(layer, kind, th, k).wait_recv()
        for k in range(5):
            rs_copy(layer, kind, th, k).wait_send()

    def pair_out(layer, hh, th):
        rs_wait(layer, hh, th)
        part[th, hh, 1, x, c] = part[th, hh, 1, x, c] + t3[th, hh, 1, 0] + t3[th, hh, 1, 1]
        pair_sums(layer, th, hh).start()

    def add_residual(th, paired):
        for b in BOTH:
            r = _cut(b, 16)
            s = [part[th, hh, 0, x, c, r] + t3[th, hh, 0, 0, r] + t3[th, hh, 0, 1, r] for hh in BOTH]
            if paired:
                s = [s[hh] + t4[th, hh, r] for hh in BOTH]
            cols = [s[hh][:, f * LANE:(f + 1) * LANE] for f in range(16) for hh in BOTH]
            res[th, r] = (res[th, r].astype(jnp.float32) + jnp.concatenate(cols, axis=1)).astype(jnp.bfloat16)

    def norm_into(th, slot, gain):
        for b in BOTH:
            r = _cut(b, 16)
            v = res[th, r].astype(jnp.float32)
            ms = jnp.mean(v * v, axis=-1, keepdims=True)
            hu[th, slot, m_me, r] = (v * lax.rsqrt(ms + EPS) * gain).astype(jnp.bfloat16)

    def src_all(rel):
        return lax.rem(z + lax.div(rel, RING), RING) * RING + lax.rem(y + lax.rem(rel, RING), RING)

    def src_split(rel):
        role = lax.rem(rel, RING)
        b = y + lax.rem(role, 2) * (y_next - y)
        return lax.rem(z + lax.div(rel, RING), RING) * RING + b + lax.div(role, 2) * (3 - 2 * b)

    def load_unit(g, n, slot, own, where):
        mine = wbuf.at[slot, f_me]
        if len(own) == 1:
            pltpu.make_async_copy(own[0], mine, w_sem.at[slot]).start()
        else:
            for k in BOTH:
                pltpu.make_async_copy(own[k], mine.at[:, :, :, pl.ds(k * LANE, LANE)], w_sem.at[slot]).start()

        def one(rel, _):
            pltpu.make_async_copy(g.at[n, rel], wbuf.at[slot, where(rel)], w_sem.at[slot]).start()
            return 0
        lax.fori_loop(1, 16, one, 0)

    def wait_unit(slot):
        pltpu.make_async_copy(wbuf.at[slot], wbuf.at[slot], w_sem.at[slot]).wait()

    def load_down(layer, hh):
        for r in BOTH:
            k = 2 * hh + r
            pltpu.make_async_copy(own_dn(layer, k, side), dbuf.at[r, :, :, :, lanes(f_me)], d_sem).start()

            def one(rel, _):
                pltpu.make_async_copy(dn_g.at[layer * N_DN + k, rel], dbuf.at[r, :, :, :, lanes(src_split(rel))], d_sem).start()
                return 0
            lax.fori_loop(1, 16, one, 0)

    def project(lhs, ws):
        return jnp.dot(lhs, wbuf[ws].reshape(WIDE, UNIT), preferred_element_type=jnp.float32)

    def rope_store(lane, dst):
        v = acc[0:GRP, lane:lane + LANE].astype(jnp.bfloat16).astype(jnp.float32)
        dst[...] = (v * cos_ref[...] + pltpu.roll(v, TOK, 1) * sin_ref[...]).astype(jnp.bfloat16)

    def load_qkv(layer):
        base = layer * N_AT
        for u in BOTH:
            load_unit(at_g, base + u, u, [own_unit(wq, layer, u)], src_all)
        load_unit(at_g, base + KV, KV, [wk.at[layer], wv.at[layer]], src_all)

    def qkv(layer, th):
        for u in range(KV + 1):
            wait_unit(u)
            acc[0:GRP] = project(hu[th, 0].reshape(GRP, WIDE), u)
            if u < KV:
                load_unit(at_g, layer * N_AT + O_ITEM + u, u, [wo.at[layer, u]], src_all)
                for h in BOTH:
                    rope_store(h * LANE, qbuf.at[2 * u + h])
        rope_store(0, kbuf)
        vbuf[...] = acc[0:GRP, LANE:].astype(jnp.bfloat16)

    def attention():
        qi = lax.broadcasted_iota(jnp.int32, (GRP, GRP), 0)
        ki = lax.broadcasted_iota(jnp.int32, (GRP, GRP), 1)
        same = ((qi >> 3) & 3) == ((ki >> 3) & 3)
        qpos = (qi >> 5) * 8 + (qi & 7)
        kpos = (ki >> 5) * 8 + (ki & 7)
        ok = jnp.logical_and(same, qpos >= kpos)
        for h in range(RING):
            s = lax.dot_general(qbuf[h], kbuf[...], (((1,), (1,)), ((), ())), preferred_element_type=jnp.float32)
            s = jnp.where(ok, s * HEAD_SCALE, -jnp.inf)
            e = jnp.exp(s - jnp.max(s, axis=-1, keepdims=True))
            p = (e / jnp.sum(e, axis=-1, keepdims=True)).astype(jnp.bfloat16)
            o = jnp.dot(p, vbuf[...], preferred_element_type=jnp.float32)
            obuf[:, h * LANE:(h + 1) * LANE] = o.astype(jnp.bfloat16)

    def cols_of(f):
        return pl.ds(pl.multiple_of(f * UNIT, UNIT), UNIT)

    def out_proj(th):
        for u in BOTH:
            wait_unit(u)

        def step(i, _):
            for e in range(RING):
                f = i * RING + e
                out = sum(jnp.dot(obuf[:, u * UNIT:(u + 1) * UNIT], wbuf[u, f].reshape(UNIT, UNIT), preferred_element_type=jnp.float32) for u in BOTH)
                for hh in BOTH:
                    part[th, hh, 0, :, :, :, lanes(f)] = out[:, hh * LANE:(hh + 1) * LANE].reshape(RING, 2, SUB, LANE)
            return 0
        lax.fori_loop(0, RING, step, 0)

    def load_gu(layer, j):
        load_unit(gu_g, layer * N_GU + j, j % 2 if isinstance(j, int) else 0, [own_gu(wg, layer, j, side), own_gu(wu, layer, j, side)], src_split)

    def gate_up(layer, j0, j1, th):
        for j in range(j0, j1):
            if j + 1 < j1:
                load_gu(layer, j + 1)
            wait_unit(j % 2)
            acc[...] = project(hu[th, 1:3].reshape(ROWS, WIDE), j % 2)
            zbuf[th, :, j * LANE:(j + 1) * LANE] = (jax.nn.silu(acc[:, 0:LANE]) * acc[:, LANE:]).astype(jnp.bfloat16)
        if th == 0:
            load_gu(layer, jnp.where((layer == 1) == (j0 == 0), RING, 0))
        elif j1 < N_GU:
            load_gu(layer, RING)

    def down(th, hh):
        def step(n, _):
            rhs = dbuf[:, :, :, :, cols_of(n)].reshape(HID, UNIT)
            out = jnp.dot(zbuf[th], rhs, preferred_element_type=jnp.float32)
            part[th, hh, :, :, :, :, cols_of(n)] = out.reshape(2, RING, 2, SUB, UNIT)
            return 0
        lax.fori_loop(0, 8, step, 0)

    barrier = pltpu.get_barrier_semaphore()
    peers = [dev_of[a, s] for a in BOTH for s in SIGNS] + [dev_xu, dev_xd, dev_sib]
    for dev in peers:
        pl.semaphore_signal(barrier, inc=1, device_id=dev, device_id_type=MESH)
    pl.semaphore_wait(barrier, len(peers))

    def every(fn):
        lax.fori_loop(0, N_AT, lambda n, _: (fn(n), 0)[1], 0)

    every(start_own)
    for th in BOTH:
        res[th] = x_ref[th]
        norm_into(th, 0, ga_ref[0])
        ag_start(0, 0, th)
    for stage in range(1, RING):
        every(lambda n: serve("at", n, stage))
        if stage == 1:
            for th in BOTH:
                ag_mid(0, 0, th)
        if stage == FAR:
            for k in range(AHEAD):
                start_own(N_AT + k)
    every(lambda n: serve("at", n, RING))

    def attend(l, th):
        ag_end(l, 0, th)
        qkv(l, th)
        attention()
        out_proj(th)
        rs_copy(l, 2, th, 0).start()
        if th == 0:
            load_qkv(l)

    def to_mlp(l, th):
        rs_wait(l, 2, th)
        add_residual(th, False)
        norm_into(th, 1, gm_ref[l])
        pair_tokens(l, th).start()
        ag_start(l, 1, th)

    def mlp_mid(l, th):
        ag_mid(l, 1, th)
        pair_tokens(l, th).wait()
        ag_start(l, 2, th)

    def mlp_far(l, th):
        ag_end(l, 1, th)
        ag_mid(l, 2, th)
        if th == 0:
            load_gu(l, 0)

    def mlp_in(l, j0, j1, th):
        if j0 == 0:
            ag_end(l, 2, th)
        gate_up(l, j0, j1, th)

    def mlp_out(l, hh, th):
        if th == 0:
            load_down(l, hh)
            pltpu.make_async_copy(dbuf, dbuf, d_sem).wait()
        down(th, hh)
        rs_copy(l, hh, th, 0).start()

    def finish(l, th):
        for hh in BOTH:
            pair_sums(l, th, hh).wait()
        add_residual(th, True)

        @pl.when(l == 0)
        def _():
            norm_into(th, 0, ga_ref[1])
            ag_start(1, 0, th)

    def ag_next(l, th):
        @pl.when(l == 1)
        def _():
            ag_mid(1, 0, th)
        if th == 0:
            load_qkv(l)

    hooks = [
        ("90 93 150 152", finish),
        ("78 82 143 144", lambda l, th: pair_out(l, 0, th)),
        ("87 90 148 149", lambda l, th: pair_out(l, 1, th)),
        ("72 75 135 137", lambda l, th: rs_near(l, 0, th)),
        ("81 84 145 146", lambda l, th: rs_near(l, 1, th)),
        ("69 71 132 135", lambda l, th: rs_far(l, 0, th)),
        ("78 80 141 142", lambda l, th: rs_far(l, 1, th)),
        ("67 69 131 132", lambda l, th: mlp_out(l, 0, th)),
        ("75 77 139 140", lambda l, th: mlp_out(l, 1, th)),
        ("50 53 122 127", lambda l, th: mlp_in(l, 0, 4, th)),
        ("41 46 119 125", mlp_far),
        ("59 62 125 129", lambda l, th: mlp_in(l, 4, 7, th)),
        ("37 42 114 121", mlp_mid),
        ("33 38 109 117", to_mlp),
        ("28 33 103 111", lambda l, th: rs_near(l, 2, th)),
        ("24 29 101 104", lambda l, th: rs_far(l, 2, th)),
        ("20 20 95 97", ag_next),
        ("20 24 98 101", attend),
    ]

    def step(t, _):
        tick(t)
        for when, what in hooks:
            u = [int(n) for n in when.split()]
            for th in BOTH:
                @pl.when(jnp.logical_or(t == u[th], t == u[FAR + th]))
                def _():
                    what(jnp.where(t == u[FAR + th], 1, 0), th)
        return 0
    lax.fori_loop(RING * N_AT, 154, step, 0)
    y_ref[...] = res[...]

    for plan, g, _, send in kinds.values():
        def drain(n, _):
            span = g.at[n, pl.ds(0, 15)]
            pltpu.make_async_copy(span, span, send.at[n]).wait()
            return 0
        lax.fori_loop(0, g.shape[0], drain, 0)


def _call(x, ga, gm, cos, sin, *weights):
    bf, f32 = jnp.bfloat16, jnp.float32
    vm = pl.BlockSpec(memory_space=pltpu.VMEM)
    anys = pl.BlockSpec(memory_space=pl.ANY)
    dma = pltpu.SemaphoreType.DMA
    n_at, n_gu, n_dn = 2 * N_AT, 2 * N_GU, 2 * N_DN
    unit = (16, 2, 2, TOK, UNIT)
    return pl.pallas_call(
        body,
        out_shape=(jax.ShapeDtypeStruct((2, SUB, WIDE), bf), jax.ShapeDtypeStruct((n_at, *unit), bf),
                   jax.ShapeDtypeStruct((n_gu, *unit), bf), jax.ShapeDtypeStruct((n_dn, 16, 2, 2, DROW, LANE), bf)),
        in_specs=[vm] * 5 + [anys] * len(weights),
        out_specs=(vm, anys, anys, anys),
        scratch_shapes=[
            pltpu.VMEM((2, 3, 8, SUB, WIDE), bf),
            pltpu.VMEM((3, *unit), bf),
            pltpu.VMEM((2, 2, 2, DROW, HALF), bf),
            pltpu.VMEM((2, 2, 2, RING, 2, SUB, HALF), f32),
            pltpu.VMEM((2, 2, 2, RING, SUB, HALF), f32),
            pltpu.VMEM((2, 2, 2, 2, SUB // 2, HALF), f32),
            pltpu.VMEM((2, 2, 2, 2, SUB, HALF), f32),
            pltpu.VMEM((2, 2, SUB, HALF), f32),
            pltpu.VMEM((2, ROWS, HID), bf),
            pltpu.VMEM((RING, GRP, LANE), bf),
            pltpu.VMEM((GRP, LANE), bf),
            pltpu.VMEM((GRP, LANE), bf),
            pltpu.VMEM((GRP, ROWS), bf),
            pltpu.VMEM((2, SUB, WIDE), bf),
            pltpu.VMEM((ROWS, UNIT), f32),
            dma((n_at, len(ALL))), dma((n_gu, len(SPLIT))), dma((n_dn, len(SPLIT))),
            dma((n_at,)), dma((n_gu,)), dma((n_dn,)),
            dma((2, 3, 2, 8)), dma((2, 3, 2, 8)), dma((2, 3, 2, 5)), dma((2, 3, 2, 5)), dma((2, 2, 3)), dma((2, 2, 3)), dma((3,)), dma,
        ],
        compiler_params=pltpu.CompilerParams(collective_id=0, has_side_effects=True, vmem_limit_bytes=63 * 1024 * 1024),
        cost_estimate=pl.CostEstimate(flops=56 * 10 ** 9, bytes_accessed=330 * 10 ** 6, transcendentals=10 ** 7),
    )(x, ga, gm, cos, sin, *weights)[0]


def solution(mesh):
    act = P('fsdp', 'model', None)
    col = P(None, 'fsdp', 'model')
    row = P(None, 'model', 'fsdp')

    def device_step(x_in, gain_attn, gain_mlp, rope_cos, rope_sin, w_q, w_k, w_v, w_o, w_gate, w_up, w_down):
        def rows_of(t):
            return jnp.broadcast_to(t.reshape(8, 1, 8, TOK), (8, RING, 8, TOK)).reshape(GRP, TOK)

        cos, sin = rows_of(rope_cos), rows_of(rope_sin)
        cos2 = jnp.concatenate([cos, cos], axis=1)
        sin2 = jnp.concatenate([-sin, sin], axis=1)
        def quarters(w):
            return w.reshape(w.shape[0], 2, 2, TOK, -1)


        y = _call(x_in.reshape(2, SUB, WIDE), gain_attn.reshape(2, 1, WIDE), gain_mlp.reshape(2, 1, WIDE), cos2, sin2,
                  quarters(w_q), quarters(w_k), quarters(w_v), w_o.reshape(2, 2, 2, 2, TOK, UNIT), quarters(w_gate), quarters(w_up), w_down.reshape(2, 2, 2, 2, 2, DROW, UNIT))
        return y.reshape(x_in.shape)

    return jax.shard_map(device_step, mesh=mesh, in_specs=(act, P(), P(), P(), P(), col, col, col, row, col, col, row), out_specs=act, check_vma=False)
```

time: 619 us -> 549 us (0.89)
  Pallas kernels: 610 us -> 540 us
    pallas_call x1, Pallas kernels: 610 us -> 540 us  [_call(): pl.pallas_call(body, out_shape=(jax.ShapeDtypeStruct((2, SUB, WIDE), bf),...]
where the time goes in v3:
time: 549 us; the launch traced here: 548 us
  Pallas kernels  540 us (98%)
  local copies, waits for them, and re-layouts  6.17 us (1%)
    pallas_call x1, Pallas kernels, _call(): pl.pallas_call(body, out_shape=(jax.ShapeDtypeStruct((2, SUB, WIDE), bf),...  540 us

profile of v3, /device:TPU:1, one launch (start us, length us, event | category | flops | bytes accessed | tf_op | source)
XLA Modules:
  0.0 547.7 jit_solution(2090793928865514370)
XLA Ops:
  0.0 1.4 reshape.44.ga_ref
  1.4 1.4 reshape.45.gm_ref
  2.8 0.8 broadcast_in_dim.15
  3.5 0.8 bitcast_negate_fusion
  4.3 0.8 broadcast_in_dim.17
  5.1 0.8 pad_maximum_fusion
  5.9 539.9 %shard_map.118 = (bf16[2,32,4096]{2,1,0:T(8,128)(2,1)}, bf16[10,16,2,2,64,256]{5,4,3,2,1,0:T(8,128)(2,1)}, bf16[14,16,2,2,64,256]{5,4,3,2,1,0:T(8,128)(2,1)}, bf16[8,16,2,2,112,128]{5,4,3,2,1,0:T(8,128)(2,1)}) custom-call(bf16[2,32,4096]{2,1,0:T(8,128)(2,1)} %bitcast.23, f32[2,1,4096]{2,1,0:T(1,128)} %reshape.44.ga_ref, f32[2,1,4096]{2,1,0:T(1,128)} %reshape.45.gm_ref, ...), custom_call_target="tpu_custom_call" | custom-call | flops 56000000000 | bytes 330000000 | tf_op jit(solution)/shard_map/pallas_call | solution.py:565
  545.9 1.9 copy.14

commit v4 on v3

--- a/solution.py
+++ b/solution.py
@@ -102,9 +102,9 @@
     return FULL if n is None else pl.ds(n * size, size)
 
 
-def body(x_ref, ga_ref, gm_ref, cos_ref, sin_ref, wq, wk, wv, wo, wg, wu, wd, y_ref, at_g, gu_g, dn_g,
-         hu, wbuf, dbuf, part, t1, t2, t3, t4, zbuf, qbuf, kbuf, vbuf, obuf, res, acc,
-         at_recv, gu_recv, dn_recv, at_send, gu_send, dn_send, ag_recv, ag_send, rs_recv, rs_send, pr_recv, pr_send, w_sem, d_sem):
+def body(x_ref, ga_ref, gm_ref, cos_in, sin_in, wq, wk, wv, wo, wg, wu, wd, y_ref, at_g, gu_g, dn_g,
+         hu, wbuf, dbuf, part, t1, t2, t3, t4, t5, cos_ref, sin_ref, zbuf, qbuf, kbuf, vbuf, obuf, res, acc,
+         at_recv, gu_recv, dn_recv, at_send, gu_send, dn_send, ag_recv, ag_send, rs_recv, rs_send, pr_recv, pr_send, sw_recv, sw_send, w_sem, d_sem):
     f_me = lax.axis_index("fsdp")
     m_me = lax.axis_index("model")
     z, y = lax.div(f_me, RING), lax.rem(f_me, RING)
@@ -130,12 +130,22 @@
 
     kinds = {"at": (ALL, at_g, at_recv, at_send), "gu": (SPLIT, gu_g, gu_recv, gu_send), "dn": (SPLIT, dn_g, dn_recv, dn_send)}
 
-    def stream_copy(kind, n, i):
+    y_of = {"at": [lax.rem(y + k, RING) for k in range(RING)], "gu": [y, y_next, 3 - y, 3 - y_next]}
+    y_of["dn"] = y_of["gu"]
+
+    def slot_of(kind, seen, src):
+        return seen // RING * RING + y_of[kind][src % RING]
+
+    def stream_copy(kind, n, i, land=False):
         plan, g, recv, send = kinds[kind]
         p = plan[i]
         a, b = _cut(p["sub"], 1), _cut(p["half"], 1)
-        at = p["src"] if p["stage"] else p["dst"]
-        return remote(g.at[n, at, a, b], g.at[n, p["dst"], a, b], send.at[n], recv.at[n, i], dev_of[p["way"]])
+        dst = g.at[n, slot_of(kind, p["dst"], p["dst"] if land else p["src"]), a, b]
+        src = dst if land else g.at[n, slot_of(kind, p["src"], p["src"]), a, b]
+        return remote(src, dst, send.at[n], recv.at[n, i], dev_of[p["way"]])
+
+    def landed(kind, n, i):
+        stream_copy(kind, n, i, True).wait_recv()
 
     def own_unit(w, layer, j):
         return w.at[layer, :, :, :, pl.ds(pl.multiple_of(j * UNIT, UNIT), UNIT)]
@@ -153,7 +163,7 @@
             plan, g, recv, sems = kinds[kind]
             for i in _of(plan, 0):
                 way = plan[i]["way"]
-                dst = g.at[n, plan[i]["dst"]]
+                dst = g.at[n, slot_of(kind, plan[i]["dst"], 0)]
                 if lane is not None:
                     dst = dst.at[:, :, :, pl.ds(lane, LANE)]
                 remote(src(1 - side if way == "pair" else side), dst, sems.at[n], recv.at[n, i], dev_of[way]).start()
@@ -189,12 +199,12 @@
         for i in _of(plan, stage):
             for j in before:
                 if j not in waited and plan[j]["dst"] == plan[i]["src"] and plan[j]["q"] & plan[i]["q"]:
-                    stream_copy(kind, n, j).wait_recv()
+                    landed(kind, n, j)
                     waited.add(j)
             stream_copy(kind, n, i).start()
         for j in before:
             if j not in waited:
-                stream_copy(kind, n, j).wait_recv()
+                landed(kind, n, j)
 
     def forward(item, stage):
         layer, pos = lax.div(item, PER_LAYER), lax.rem(item, PER_LAYER)
@@ -258,7 +268,26 @@
         return remote(part.at[th, hh, 1, x, c], t4.at[th, hh], pr_send.at[layer, th, hh], pr_recv.at[layer, th, hh], dev_of["pair"])
 
     def spans(kind):
-        return (BOTH, (0,)) if kind == 2 else ((kind,), BOTH)
+        return [((0,), BOTH), ((1,), BOTH), (BOTH, (0,)), ((1,), (0,))][kind]
+
+    def swap():
+        return remote(part.at[1, 1, 1, :, c], t5, sw_send.at[0], sw_recv.at[0], dev_of["pair"])
+
+    def swap_out(layer):
+        rs_copy(layer, 1, 1, 0).wait_recv()
+        for g in (1, 0):
+            for xp in range(RING):
+                part[1, 1, g, xp, c] = part[1, 1, g, xp, c] + t1[1, 1, g, xp]
+            if g:
+                swap().start()
+
+    def swap_in(layer):
+        swap().wait()
+        t4[1, 1] = jnp.zeros_like(t4[1, 1])
+        for xp in (x_far, x_up, x_dn, x):
+            part[1, 1, 0, xp, c] = part[1, 1, 0, xp, c] + t5[xp]
+        for k in (1, 2):
+            rs_copy(layer, 3, 1, k).start()
 
     def rs_copy(layer, kind, th, k):
         hs, gs = spans(kind)
@@ -299,7 +328,7 @@
         for k in (3, 4):
             rs_copy(layer, kind, th, k).wait_recv()
         for k in range(5):
-            rs_copy(layer, kind, th, k).wait_send()
+            rs_copy(layer, 1 if kind == 3 and k == 0 else kind, th, k).wait_send()
 
     def pair_out(layer, hh, th):
         rs_wait(layer, hh, th)
@@ -322,26 +351,23 @@
             ms = jnp.mean(v * v, axis=-1, keepdims=True)
             hu[th, slot, m_me, r] = (v * lax.rsqrt(ms + EPS) * gain).astype(jnp.bfloat16)
 
-    def src_all(rel):
-        return lax.rem(z + lax.div(rel, RING), RING) * RING + lax.rem(y + lax.rem(rel, RING), RING)
-
-    def src_split(rel):
-        role = lax.rem(rel, RING)
-        b = y + lax.rem(role, 2) * (y_next - y)
-        return lax.rem(z + lax.div(rel, RING), RING) * RING + b + lax.div(role, 2) * (3 - 2 * b)
-
-    def load_unit(g, n, slot, own, where):
+    def place(rel):
+        yk = lax.rem(y + lax.rem(rel, RING), RING)
+        dz = lax.div(rel, RING)
+        return dz * RING + yk, lax.rem(z + dz, RING) * RING + yk
+
+    def load_unit(g, n, slot, own):
         mine = wbuf.at[slot, f_me]
         if len(own) == 1:
             pltpu.make_async_copy(own[0], mine, w_sem.at[slot]).start()
         else:
             for k in BOTH:
                 pltpu.make_async_copy(own[k], mine.at[:, :, :, pl.ds(k * LANE, LANE)], w_sem.at[slot]).start()
-
-        def one(rel, _):
-            pltpu.make_async_copy(g.at[n, rel], wbuf.at[slot, where(rel)], w_sem.at[slot]).start()
-            return 0
-        lax.fori_loop(1, 16, one, 0)
+        for k in range(1, RING):
+            here, there = place(k)
+            pltpu.make_async_copy(g.at[n, here], wbuf.at[slot, there], w_sem.at[slot]).start()
+            row = lax.rem(z + k, RING) * RING
+            pltpu.make_async_copy(g.at[n, pl.ds(k * RING, RING)], wbuf.at[slot, pl.ds(row, RING)], w_sem.at[slot]).start()
 
     def wait_unit(slot):
         pltpu.make_async_copy(wbuf.at[slot], wbuf.at[slot], w_sem.at[slot]).wait()
@@ -352,7 +378,8 @@
             pltpu.make_async_copy(own_dn(layer, k, side), dbuf.at[r, :, :, :, lanes(f_me)], d_sem).start()
 
             def one(rel, _):
-                pltpu.make_async_copy(dn_g.at[layer * N_DN + k, rel], dbuf.at[r, :, :, :, lanes(src_split(rel))], d_sem).start()
+                here, there = place(rel)
+                pltpu.make_async_copy(dn_g.at[layer * N_DN + k, here], dbuf.at[r, :, :, :, lanes(there)], d_sem).start()
                 return 0
             lax.fori_loop(1, 16, one, 0)
 
@@ -366,15 +393,15 @@
     def load_qkv(layer):
         base = layer * N_AT
         for u in BOTH:
-            load_unit(at_g, base + u, u, [own_unit(wq, layer, u)], src_all)
-        load_unit(at_g, base + KV, KV, [wk.at[layer], wv.at[layer]], src_all)
+            load_unit(at_g, base + u, u, [own_unit(wq, layer, u)])
+        load_unit(at_g, base + KV, KV, [wk.at[layer], wv.at[layer]])
 
     def qkv(layer, th):
         for u in range(KV + 1):
             wait_unit(u)
             acc[0:GRP] = project(hu[th, 0].reshape(GRP, WIDE), u)
             if u < KV:
-                load_unit(at_g, layer * N_AT + O_ITEM + u, u, [wo.at[layer, u]], src_all)
+                load_unit(at_g, layer * N_AT + O_ITEM + u, u, [wo.at[layer, u]])
                 for h in BOTH:
                     rope_store(h * LANE, qbuf.at[2 * u + h])
         rope_store(0, kbuf)
@@ -412,7 +439,7 @@
         lax.fori_loop(0, RING, step, 0)
 
     def load_gu(layer, j):
-        load_unit(gu_g, layer * N_GU + j, j % 2 if isinstance(j, int) else 0, [own_gu(wg, layer, j, side), own_gu(wu, layer, j, side)], src_split)
+        load_unit(gu_g, layer * N_GU + j, j % 2 if isinstance(j, int) else 0, [own_gu(wg, layer, j, side), own_gu(wu, layer, j, side)])
 
     def gate_up(layer, j0, j1, th):
         for j in range(j0, j1):
@@ -446,8 +473,14 @@
     every(start_own)
     for th in BOTH:
         res[th] = x_ref[th]
-        norm_into(th, 0, ga_ref[0])
+        norm_into(th, 0, ga_ref[0:1])
         ag_start(0, 0, th)
+    for i in range(8):
+        co, si = cos_in[i * 8:(i + 1) * 8], sin_in[i * 8:(i + 1) * 8]
+        for b in range(RING):
+            r = pl.ds(i * SUB + b * 8, 8)
+            cos_ref[r] = jnp.concatenate([co, co], axis=1)
+            sin_ref[r] = jnp.concatenate([-si, si], axis=1)
     for stage in range(1, RING):
         every(lambda n: serve("at", n, stage))
         if stage == 1:
@@ -470,7 +503,7 @@
     def to_mlp(l, th):
         rs_wait(l, 2, th)
         add_residual(th, False)
-        norm_into(th, 1, gm_ref[l])
+        norm_into(th, 1, gm_ref[pl.ds(l, 1)])
         pair_tokens(l, th).start()
         ag_start(l, 1, th)
 
@@ -498,13 +531,22 @@
         rs_copy(l, hh, th, 0).start()
 
     def finish(l, th):
-        for hh in BOTH:
-            pair_sums(l, th, hh).wait()
+        pair_sums(l, th, 0).wait()
+        if th == 0:
+            pair_sums(l, th, 1).wait()
+        else:
+            @pl.when(l == 0)
+            def _():
+                pair_sums(l, th, 1).wait()
+
+            @pl.when(l == 1)
+            def _():
+                rs_wait(l, 3, th)
         add_residual(th, True)
 
         @pl.when(l == 0)
         def _():
-            norm_into(th, 0, ga_ref[1])
+            norm_into(th, 0, ga_ref[1:2])
             ag_start(1, 0, th)
 
     def ag_next(l, th):
@@ -515,18 +557,21 @@
             load_qkv(l)
 
     hooks = [
-        ("90 93 150 152", finish),
-        ("78 82 143 144", lambda l, th: pair_out(l, 0, th)),
-        ("87 90 148 149", lambda l, th: pair_out(l, 1, th)),
-        ("72 75 135 137", lambda l, th: rs_near(l, 0, th)),
-        ("81 84 145 146", lambda l, th: rs_near(l, 1, th)),
-        ("69 71 132 135", lambda l, th: rs_far(l, 0, th)),
-        ("78 80 141 142", lambda l, th: rs_far(l, 1, th)),
-        ("67 69 131 132", lambda l, th: mlp_out(l, 0, th)),
-        ("75 77 139 140", lambda l, th: mlp_out(l, 1, th)),
-        ("50 53 122 127", lambda l, th: mlp_in(l, 0, 4, th)),
+        ("78 82 145 147", lambda l, th: pair_out(l, 0, th)),
+        ("87 90 150 0", lambda l, th: pair_out(l, 1, th)),
+        ("72 75 134 144", lambda l, th: rs_near(l, 0, th)),
+        ("81 84 146 0", lambda l, th: rs_near(l, 1, th)),
+        ("0 0 0 149", lambda l, th: rs_near(l, 3, th)),
+        ("90 93 151 152", finish),
+        ("69 71 132 140", lambda l, th: rs_far(l, 0, th)),
+        ("78 80 143 0", lambda l, th: rs_far(l, 1, th)),
+        ("0 0 0 142", lambda l, th: swap_out(l)),
+        ("0 0 0 148", lambda l, th: swap_in(l)),
+        ("67 69 131 136", lambda l, th: mlp_out(l, 0, th)),
+        ("75 77 139 141", lambda l, th: mlp_out(l, 1, th)),
+        ("50 53 122 133", lambda l, th: mlp_in(l, 0, 4, th)),
         ("41 46 119 125", mlp_far),
-        ("59 62 125 129", lambda l, th: mlp_in(l, 4, 7, th)),
+        ("59 62 125 135", lambda l, th: mlp_in(l, 4, 7, th)),
         ("37 42 114 121", mlp_mid),
         ("33 38 109 117", to_mlp),
         ("28 33 103 111", lambda l, th: rs_near(l, 2, th)),
@@ -539,7 +584,7 @@
         tick(t)
         for when, what in hooks:
             u = [int(n) for n in when.split()]
-            for th in BOTH:
+            for th in [h for h in BOTH if u[h] or u[FAR + h]]:
                 @pl.when(jnp.logical_or(t == u[th], t == u[FAR + th]))
                 def _():
                     what(jnp.where(t == u[FAR + th], 1, 0), th)
@@ -577,6 +622,9 @@
             pltpu.VMEM((2, 2, 2, 2, SUB // 2, HALF), f32),
             pltpu.VMEM((2, 2, 2, 2, SUB, HALF), f32),
             pltpu.VMEM((2, 2, SUB, HALF), f32),
+            pltpu.VMEM((RING, SUB, HALF), f32),
+            pltpu.VMEM((GRP, LANE), f32),
+            pltpu.VMEM((GRP, LANE), f32),
             pltpu.VMEM((2, ROWS, HID), bf),
             pltpu.VMEM((RING, GRP, LANE), bf),
             pltpu.VMEM((GRP, LANE), bf),
@@ -586,7 +634,7 @@
             pltpu.VMEM((ROWS, UNIT), f32),
             dma((n_at, len(ALL))), dma((n_gu, len(SPLIT))), dma((n_dn, len(SPLIT))),
             dma((n_at,)), dma((n_gu,)), dma((n_dn,)),
-            dma((2, 3, 2, 8)), dma((2, 3, 2, 8)), dma((2, 3, 2, 5)), dma((2, 3, 2, 5)), dma((2, 2, 3)), dma((2, 2, 3)), dma((3,)), dma,
+            dma((2, 3, 2, 8)), dma((2, 3, 2, 8)), dma((2, RING, 2, 5)), dma((2, RING, 2, 5)), dma((2, 2, 3)), dma((2, 2, 3)), dma((1,)), dma((1,)), dma((3,)), dma,
         ],
         compiler_params=pltpu.CompilerParams(collective_id=0, has_side_effects=True, vmem_limit_bytes=63 * 1024 * 1024),
         cost_estimate=pl.CostEstimate(flops=56 * 10 ** 9, bytes_accessed=330 * 10 ** 6, transcendentals=10 ** 7),
@@ -599,17 +647,11 @@
     row = P(None, 'model', 'fsdp')
 
     def device_step(x_in, gain_attn, gain_mlp, rope_cos, rope_sin, w_q, w_k, w_v, w_o, w_gate, w_up, w_down):
-        def rows_of(t):
-            return jnp.broadcast_to(t.reshape(8, 1, 8, TOK), (8, RING, 8, TOK)).reshape(GRP, TOK)
-
-        cos, sin = rows_of(rope_cos), rows_of(rope_sin)
-        cos2 = jnp.concatenate([cos, cos], axis=1)
-        sin2 = jnp.concatenate([-sin, sin], axis=1)
         def quarters(w):
             return w.reshape(w.shape[0], 2, 2, TOK, -1)
 
 
-        y = _call(x_in.reshape(2, SUB, WIDE), gain_attn.reshape(2, 1, WIDE), gain_mlp.reshape(2, 1, WIDE), cos2, sin2,
+        y = _call(x_in.reshape(2, SUB, WIDE), gain_attn, gain_mlp, rope_cos, rope_sin,
                   quarters(w_q), quarters(w_k), quarters(w_v), w_o.reshape(2, 2, 2, 2, TOK, UNIT), quarters(w_gate), quarters(w_up), w_down.reshape(2, 2, 2, 2, 2, DROW, UNIT))
         return y.reshape(x_in.shape)
 

time: 549 us -> 524 us (0.954)
  Pallas kernels: 540 us -> 521 us
    pallas_call x1, Pallas kernels: 540 us -> 521 us  [_call(): pl.pallas_call(body, out_shape=(jax.ShapeDtypeStruct((2, SUB, WIDE), bf),...]
where the time goes in v4:
time: 524 us; the launch traced here: 523 us
  Pallas kernels  521 us (99%)
    pallas_call x1, Pallas kernels, _call(): pl.pallas_call(body, out_shape=(jax.ShapeDtypeStruct((2, SUB, WIDE), bf),...  521 us

profile of v4, /device:TPU:1, one launch (start us, length us, event | category | flops | bytes accessed | tf_op | source)
XLA Modules:
  0.0 523.3 jit_solution(7045573677477490153)
XLA Ops:
  0.0 521.4 %shard_map.118 = (bf16[2,32,4096]{2,1,0:T(8,128)(2,1)}, bf16[10,16,2,2,64,256]{5,4,3,2,1,0:T(8,128)(2,1)}, bf16[14,16,2,2,64,256]{5,4,3,2,1,0:T(8,128)(2,1)}, bf16[8,16,2,2,112,128]{5,4,3,2,1,0:T(8,128)(2,1)}) custom-call(bf16[2,32,4096]{2,1,0:T(8,128)(2,1)} %bitcast.13, f32[2,4096]{1,0:T(2,128)} %ga_ref.1, f32[2,4096]{1,0:T(2,128)} %gm_ref.1, ...), custom_call_target="tpu_custom_call" | custom-call | flops 56000000000 | bytes 330000000 | tf_op jit(solution)/shard_map/pallas_call | solution.py:610
  521.4 1.9 copy.14
